TPU v7x, 32 devices: a whole 2x2x4 slice. The times are simulated.
32 devices in a mesh: rep: 16 (over z, y, core), shard: 2 (over x).
Axes of the slice: x: 2, y: 2, z: 4, core: 2. Of those that a mesh axis runs over, the one named last changes fastest.
Arguments:
- tokens: bfloat16 [32768, 768], P(('rep', 'shard')), may hold values from -6 to 6
- ln1_gain: bfloat16 [768], P('shard'), may hold values from 0.5 to 1.5
- ln1_bias: bfloat16 [768], P('shard'), may hold values from -1.5 to 1.5
- qkv_weight: bfloat16 [768, 2304], P('shard'), may hold values from -0.21875 to 0.21875
- qv_bias: bfloat16 [1536], P('shard'), may hold values from -1.5 to 1.5
- proj_weight: bfloat16 [768, 768], P('shard'), may hold values from -0.875 to 0.875
- proj_bias: bfloat16 [768], P('shard'), may hold values from -1.5 to 1.5
- ln2_gain: bfloat16 [768], P('shard'), may hold values from 0.5 to 1.5
- ln2_bias: bfloat16 [768], P('shard'), may hold values from -1.5 to 1.5
- fc_weight: bfloat16 [768, 3072], P('shard'), may hold values from -0.21875 to 0.21875
- fc_bias: bfloat16 [3072], P('shard'), may hold values from -1.5 to 1.5
- out_weight: bfloat16 [3072, 768], P('shard'), may hold values from -0.15625 to 0.15625
- out_bias: bfloat16 [768], P('shard'), may hold values from -1.5 to 1.5
- cotangent: bfloat16 [32768, 768], P(('rep', 'shard')), may hold values from -6 to 6
Outputs:
- block_out: bfloat16 [32768, 768], P(('rep', 'shard'))
- input_gradient: bfloat16 [32768, 768], P(('rep', 'shard'))
- ln1_gain_grad: float32 [768], P('shard')
- ln1_bias_grad: float32 [768], P('shard')
- qkv_weight_grad: float32 [768, 2304], P('shard')
- qv_bias_grad: float32 [1536], P('shard')
- proj_weight_grad: float32 [768, 768], P('shard')
- proj_bias_grad: float32 [768], P('shard')
- ln2_gain_grad: float32 [768], P('shard')
- ln2_bias_grad: float32 [768], P('shard')
- fc_weight_grad: float32 [768, 3072], P('shard')
- fc_bias_grad: float32 [3072], P('shard')
- out_weight_grad: float32 [3072, 768], P('shard')
- out_bias_grad: float32 [768], P('shard')
All inputs are finite; a program needn't handle non-finite values.
Results may differ from a plain program's by a relative error of at most 0.018.
Values may be sent and summed in bfloat16 or wider, within the bound.
A program may use at most 256 MiB of HBM per device.

v0:
```python
import jax
import jax.numpy as jnp
from jax import lax
from jax.sharding import PartitionSpec as P

HEADS = 12
HEAD_DIM = 64
SEQ_LEN = 512


EPS = 1e-05
GELU_C = 0.7978845608028654


def layer_norm_rows(value_rows):
    center = value_rows - jnp.mean(value_rows, axis=-1, keepdims=True)
    inverse_deviation = lax.rsqrt(jnp.mean(center * center, axis=-1, keepdims=True) + EPS)
    return (center * inverse_deviation, inverse_deviation)


def causal_scores(query_rows, key_portion):
    scores = jnp.einsum(
        "sqhd,skhd->shqk", query_rows, key_portion, preferred_element_type=jnp.float32
    ) * HEAD_DIM ** (-0.5)
    rows = lax.broadcasted_iota(jnp.int32, (SEQ_LEN, SEQ_LEN), 0)
    cols = lax.broadcasted_iota(jnp.int32, (SEQ_LEN, SEQ_LEN), 1)
    return jnp.where(cols <= rows, scores, -1e30)


def forward(tokens, params):
    (
        first_norm_gain,
        first_norm_bias,
        wqkv,
        bqv,
        wproj,
        bproj,
        second_norm_gain,
        second_norm_bias,
        wfc,
        bfc,
        wout,
        bout,
    ) = params
    width = tokens.shape[1]
    seqs = tokens.shape[0] // SEQ_LEN
    input_wide = tokens.astype(jnp.float32)
    first_centered_normalized, first_inverse_deviation = layer_norm_rows(input_wide)
    first_normalized = (
        first_centered_normalized * first_norm_gain.astype(jnp.float32)
        + first_norm_bias.astype(jnp.float32)
    ).astype(jnp.bfloat16)
    bias_full = jnp.concatenate(
        [
            bqv[:width].astype(jnp.float32),
            jnp.zeros((width,), jnp.float32),
            bqv[width:].astype(jnp.float32),
        ]
    )
    qkv = (jnp.dot(first_normalized, wqkv, preferred_element_type=jnp.float32) + bias_full).astype(
        jnp.bfloat16
    )
    qkv = qkv.reshape(seqs, SEQ_LEN, 3, HEADS, HEAD_DIM)
    query_rows, key_portion, value_rows = (qkv[:, :, 0], qkv[:, :, 1], qkv[:, :, 2])
    scores = causal_scores(query_rows, key_portion)
    top = jnp.max(scores, axis=-1, keepdims=True)
    log_sum_exponent = top + jnp.log(jnp.sum(jnp.exp(scores - top), axis=-1, keepdims=True))
    probs = jnp.exp(scores - log_sum_exponent).astype(jnp.bfloat16)
    attention_result = jnp.einsum(
        "shqk,skhd->sqhd", probs, value_rows, preferred_element_type=jnp.float32
    ).astype(jnp.bfloat16)
    attention_result = attention_result.reshape(seqs * SEQ_LEN, width)
    residual_hidden = (
        input_wide
        + jnp.dot(attention_result, wproj, preferred_element_type=jnp.float32)
        + bproj.astype(jnp.float32)
    )
    second_centered_normalized, second_inverse_deviation = layer_norm_rows(residual_hidden)
    second_normalized = (
        second_centered_normalized * second_norm_gain.astype(jnp.float32)
        + second_norm_bias.astype(jnp.float32)
    ).astype(jnp.bfloat16)
    preactivation = jnp.dot(
        second_normalized, wfc, preferred_element_type=jnp.float32
    ) + bfc.astype(jnp.float32)
    tanh_term = jnp.tanh(
        GELU_C * (preactivation + 0.044715 * preactivation * preactivation * preactivation)
    )
    activation_output = (0.5 * preactivation * (1.0 + tanh_term)).astype(jnp.bfloat16)
    block_out = (
        residual_hidden
        + jnp.dot(activation_output, wout, preferred_element_type=jnp.float32)
        + bout.astype(jnp.float32)
    ).astype(jnp.bfloat16)
    saved_residuals = (
        first_centered_normalized,
        first_inverse_deviation,
        first_normalized,
        query_rows,
        key_portion,
        value_rows,
        log_sum_exponent,
        attention_result,
        second_centered_normalized,
        second_inverse_deviation,
        second_normalized,
        preactivation,
        activation_output,
    )
    return (block_out, saved_residuals)


def layer_norm_backward(normalized_gradient, norm_gain, centered_normalized, inverse_deviation):
    scaled_scores = normalized_gradient * norm_gain.astype(jnp.float32)
    return inverse_deviation * (
        scaled_scores
        - jnp.mean(scaled_scores, axis=-1, keepdims=True)
        - centered_normalized
        * jnp.mean(scaled_scores * centered_normalized, axis=-1, keepdims=True)
    )


def backward(saved_residuals, params, cotangent):
    (
        first_norm_gain,
        first_norm_bias,
        wqkv,
        bqv,
        wproj,
        bproj,
        second_norm_gain,
        second_norm_bias,
        wfc,
        bfc,
        wout,
        bout,
    ) = params
    (
        first_centered_normalized,
        first_inverse_deviation,
        first_normalized,
        query_rows,
        key_portion,
        value_rows,
        log_sum_exponent,
        attention_result,
        second_centered_normalized,
        second_inverse_deviation,
        second_normalized,
        preactivation,
        activation_output,
    ) = saved_residuals
    width = cotangent.shape[1]
    seqs = cotangent.shape[0] // SEQ_LEN
    output_gradient_wide = cotangent.astype(jnp.float32)
    out_w_grad = jnp.dot(activation_output.T, cotangent, preferred_element_type=jnp.float32)
    out_b_grad = jnp.sum(output_gradient_wide, axis=0)
    d_act = jnp.dot(cotangent, wout.T, preferred_element_type=jnp.float32)
    tanh_term = jnp.tanh(
        GELU_C * (preactivation + 0.044715 * preactivation * preactivation * preactivation)
    )
    slope = 0.5 * (1.0 + tanh_term) + 0.5 * preactivation * (
        1.0 - tanh_term * tanh_term
    ) * GELU_C * (1.0 + 0.134145 * preactivation * preactivation)
    d_pre32 = d_act * slope
    fc_b_grad = jnp.sum(d_pre32, axis=0)
    d_pre = d_pre32.astype(jnp.bfloat16)
    fc_w_grad = jnp.dot(second_normalized.T, d_pre, preferred_element_type=jnp.float32)
    second_normalized_gradient = jnp.dot(d_pre, wfc.T, preferred_element_type=jnp.float32)
    second_gain_gradient = jnp.sum(second_normalized_gradient * second_centered_normalized, axis=0)
    b2_grad = jnp.sum(second_normalized_gradient, axis=0)
    residual_gradient = output_gradient_wide + layer_norm_backward(
        second_normalized_gradient,
        second_norm_gain,
        second_centered_normalized,
        second_inverse_deviation,
    )
    d_hres_b = residual_gradient.astype(jnp.bfloat16)
    proj_w_grad = jnp.dot(attention_result.T, d_hres_b, preferred_element_type=jnp.float32)
    proj_b_grad = jnp.sum(residual_gradient, axis=0)
    d_att = jnp.dot(d_hres_b, wproj.T, preferred_element_type=jnp.float32).astype(jnp.bfloat16)
    d_att = d_att.reshape(seqs, SEQ_LEN, HEADS, HEAD_DIM)
    att4 = attention_result.reshape(seqs, SEQ_LEN, HEADS, HEAD_DIM)
    delta = jnp.einsum("sqhd,sqhd->shq", d_att, att4, preferred_element_type=jnp.float32)
    scores = causal_scores(query_rows, key_portion)
    probs32 = jnp.exp(scores - log_sum_exponent)
    probs = probs32.astype(jnp.bfloat16)
    d_value = jnp.einsum("shqk,sqhd->skhd", probs, d_att, preferred_element_type=jnp.float32)
    d_prob = jnp.einsum("sqhd,skhd->shqk", d_att, value_rows, preferred_element_type=jnp.float32)
    d_scores = (probs32 * (d_prob - delta[..., None]) * HEAD_DIM ** (-0.5)).astype(jnp.bfloat16)
    d_query = jnp.einsum(
        "shqk,skhd->sqhd", d_scores, key_portion, preferred_element_type=jnp.float32
    )
    d_key = jnp.einsum("shqk,sqhd->skhd", d_scores, query_rows, preferred_element_type=jnp.float32)
    d_qkv32 = jnp.stack([d_query, d_key, d_value], axis=2).reshape(seqs * SEQ_LEN, 3 * width)
    qv_b_grad = jnp.concatenate(
        [jnp.sum(d_qkv32[:, :width], axis=0), jnp.sum(d_qkv32[:, 2 * width :], axis=0)]
    )
    d_qkv = d_qkv32.astype(jnp.bfloat16)
    qkv_w_grad = jnp.dot(first_normalized.T, d_qkv, preferred_element_type=jnp.float32)
    first_normalized_gradient = jnp.dot(d_qkv, wqkv.T, preferred_element_type=jnp.float32)
    first_gain_gradient = jnp.sum(first_normalized_gradient * first_centered_normalized, axis=0)
    b1_grad = jnp.sum(first_normalized_gradient, axis=0)
    input_gradient = (
        residual_gradient
        + layer_norm_backward(
            first_normalized_gradient,
            first_norm_gain,
            first_centered_normalized,
            first_inverse_deviation,
        )
    ).astype(jnp.bfloat16)
    grads = (
        first_gain_gradient,
        b1_grad,
        qkv_w_grad,
        qv_b_grad,
        proj_w_grad,
        proj_b_grad,
        second_gain_gradient,
        b2_grad,
        fc_w_grad,
        fc_b_grad,
        out_w_grad,
        out_b_grad,
    )
    return (input_gradient, grads)


def per_device(
    tokens,
    ln1_gain,
    ln1_bias,
    qkv_weight,
    qv_bias,
    proj_weight,
    proj_bias,
    ln2_gain,
    ln2_bias,
    fc_weight,
    fc_bias,
    out_weight,
    out_bias,
    cotangent,
):
    params = (
        ln1_gain,
        ln1_bias,
        qkv_weight,
        qv_bias,
        proj_weight,
        proj_bias,
        ln2_gain,
        ln2_bias,
        fc_weight,
        fc_bias,
        out_weight,
        out_bias,
    )
    gathered = (
        lax.all_gather(params[0], "shard", axis=0, tiled=True),
        lax.all_gather(params[1], "shard", axis=0, tiled=True),
        lax.all_gather(params[2], "shard", axis=0, tiled=True),
        lax.all_gather(params[3], "shard", axis=0, tiled=True),
        lax.all_gather(params[4], "shard", axis=0, tiled=True),
        lax.all_gather(params[5], "shard", axis=0, tiled=True),
        lax.all_gather(params[6], "shard", axis=0, tiled=True),
        lax.all_gather(params[7], "shard", axis=0, tiled=True),
        lax.all_gather(params[8], "shard", axis=0, tiled=True),
        lax.all_gather(params[9], "shard", axis=0, tiled=True),
        lax.all_gather(params[10], "shard", axis=0, tiled=True),
        lax.all_gather(params[11], "shard", axis=0, tiled=True),
    )
    block_out, saved_residuals = forward(tokens, gathered)
    input_gradient, grads = backward(saved_residuals, gathered, cotangent)
    owned = (
        lax.psum_scatter(
            grads[0].astype(jnp.bfloat16), "shard", scatter_dimension=0, tiled=True
        ).astype(jnp.float32),
        lax.psum_scatter(
            grads[1].astype(jnp.bfloat16), "shard", scatter_dimension=0, tiled=True
        ).astype(jnp.float32),
        lax.psum_scatter(
            grads[2].astype(jnp.bfloat16), "shard", scatter_dimension=0, tiled=True
        ).astype(jnp.float32),
        lax.psum_scatter(
            grads[3].astype(jnp.bfloat16), "shard", scatter_dimension=0, tiled=True
        ).astype(jnp.float32),
        lax.psum_scatter(
            grads[4].astype(jnp.bfloat16), "shard", scatter_dimension=0, tiled=True
        ).astype(jnp.float32),
        lax.psum_scatter(
            grads[5].astype(jnp.bfloat16), "shard", scatter_dimension=0, tiled=True
        ).astype(jnp.float32),
        lax.psum_scatter(
            grads[6].astype(jnp.bfloat16), "shard", scatter_dimension=0, tiled=True
        ).astype(jnp.float32),
        lax.psum_scatter(
            grads[7].astype(jnp.bfloat16), "shard", scatter_dimension=0, tiled=True
        ).astype(jnp.float32),
        lax.psum_scatter(
            grads[8].astype(jnp.bfloat16), "shard", scatter_dimension=0, tiled=True
        ).astype(jnp.float32),
        lax.psum_scatter(
            grads[9].astype(jnp.bfloat16), "shard", scatter_dimension=0, tiled=True
        ).astype(jnp.float32),
        lax.psum_scatter(
            grads[10].astype(jnp.bfloat16), "shard", scatter_dimension=0, tiled=True
        ).astype(jnp.float32),
        lax.psum_scatter(
            grads[11].astype(jnp.bfloat16), "shard", scatter_dimension=0, tiled=True
        ).astype(jnp.float32),
    )
    totals = lax.psum(
        (
            owned[0],
            owned[1],
            owned[2],
            owned[3],
            owned[4],
            owned[5],
            owned[6],
            owned[7],
            owned[8],
            owned[9],
            owned[10],
            owned[11],
        ),
        "rep",
    )
    return (
        block_out,
        input_gradient,
        totals[0],
        totals[1],
        totals[2],
        totals[3],
        totals[4],
        totals[5],
        totals[6],
        totals[7],
        totals[8],
        totals[9],
        totals[10],
        totals[11],
    )


def solution(mesh):
    in_specs = (
        P(("rep", "shard"), None),
        P("shard"),
        P("shard"),
        P("shard", None),
        P("shard"),
        P("shard", None),
        P("shard"),
        P("shard"),
        P("shard"),
        P("shard", None),
        P("shard"),
        P("shard", None),
        P("shard"),
        P(("rep", "shard"), None),
    )
    out_specs = (
        P(("rep", "shard"), None),
        P(("rep", "shard"), None),
        P("shard"),
        P("shard"),
        P("shard", None),
        P("shard"),
        P("shard", None),
        P("shard"),
        P("shard"),
        P("shard"),
        P("shard", None),
        P("shard"),
        P("shard", None),
        P("shard"),
    )
    return jax.shard_map(
        per_device, mesh=mesh, in_specs=in_specs, out_specs=out_specs, check_vma=False
    )
```

profile of v0, /device:TPU:0, one launch (start us, length us, event | category | flops | bytes accessed | tf_op | source)
XLA Modules:
  0.0 834.3 jit_solution(3500482863781969276)
XLA Ops:
  47.2 14.7 %all-gather.13.cloned.1.call-done = bf16[768,2304]{1,0:T(8,128)(2,1)} async-done(((bf16[384,2304]{1,0:T(8,128)(2,1)}), bf16[768,2304]{1,0:T(8,128)(2,1)}) %all-gather.13.cloned.1.call-update) | async-done | bytes 3538960 | tf_op jit(solution)/shard_map/all_gather | solution.py:263
  61.9 7.8 add_convert_fusion
  69.7 6.7 copy.71
  76.4 8.8 %reshape.98 = bf16[2,512,3,12,64]{1,0,4,3,2:T(2,128)(2,1)} reshape(bf16[1024,2304]{0,1:T(8,128)(2,1)} %copy.71) | data formatting | bytes 9437184 | tf_op jit(solution)/shard_map/reshape | solution.py:63
  90.2 12.2 %fusion.1 = (f32[2,12,512]{2,1,0:T(8,128)S(1)}, f32[2,12,512,512]{2,3,1,0:T(8,128)}) fusion(pred[512,512]{0,1:T(8,128)(4,1)S(1)} %iota_compare_fusion, bf16[2,512,1,12,64]{1,0,4,3,2:T(2,128)(2,1)S(1)} %get-tuple-element.88, bf16[2,512,1,12,64]{1,0,4,3,2:T(2,128)(2,1)S(1)} %get-tuple-element.89), kind=kOutput, calls=%fused_computation.7 | convolution fusion | flops 824168448 | bytes 28622848 | tf_op jit(solution)/shard_map/sqhd,skhd->shqk/dot_general | solution.py:22
  102.3 11.1 %exponential_reduce_fusion = f32[2,12,512]{2,1,0:T(8,128)S(1)} fusion(f32[2,12,512,512]{2,3,1,0:T(8,128)} %get-tuple-element.92, f32[2,12,512]{2,1,0:T(8,128)S(1)} %get-tuple-element.91, pred[512,512]{0,1:T(8,128)(4,1)S(1)} %iota_compare_fusion), kind=kLoop, calls=%fused_computation.2 | loop fusion | flops 25153536 | bytes 25526272 | tf_op jit(solution)/shard_map/reduce_sum | solution.py:67
  113.5 11.6 %convolution_convert_fusion.3 = bf16[2,12,64,512]{3,2,1,0:T(8,128)(2,1)S(1)} fusion(bf16[2,512,1,12,64]{1,0,4,3,2:T(2,128)(2,1)S(1)} %get-tuple-element.90, f32[2,12,512,512]{2,3,1,0:T(8,128)} %get-tuple-element.92, f32[2,12,512]{2,1,0:T(8,128)S(1)} %log_add_fusion, pred[512,512]{0,1:T(8,128)(4,1)S(1)} %iota_compare_fusion), kind=kOutput, calls=%fused_computation.60 | convolution fusion | flops 831258624 | bytes 28622848 | tf_op jit(solution)/shard_map/shqk,skhd->sqhd/dot_general | solution.py:69
  133.7 16.8 %all-gather.17.cloned.1.call-done = bf16[768,3072]{1,0:T(8,128)(2,1)} async-done(((bf16[384,3072]{1,0:T(8,128)(2,1)}), bf16[768,3072]{1,0:T(8,128)(2,1)}) %all-gather.17.cloned.1.call-update) | async-done | bytes 4718608 | tf_op jit(solution)/shard_map/all_gather | solution.py:269
  150.4 11.0 %fusion.45 = f32[1024,3072]{1,0:T(8,128)} fusion(bf16[768,3072]{1,0:T(8,128)(2,1)} %all-gather.17.cloned.1.call-done, f32[1024,768]{0,1:T(8,128)S(1)} %get-tuple-element.94, f32[768]{0:T(1024)S(1)} %reshape.122, f32[768]{0:T(1024)S(1)} %reshape.121, f32[1024]{0:T(1024)S(1)} %add_rsqrt_fusion, f32[1024]{0:T(1024)S(1)} %broadcast_multiply_fusion.4), kind=kOutput, calls=%fused_computation.106 | convolution fusion | flops 4835770368 | bytes 20461568 | tf_op jit(solution)/shard_map/dot_general | solution.py:83
  161.5 53.0 %all-gather.19.cloned.1.call-done = bf16[3072,768]{1,0:T(8,128)(2,1)} async-done(((bf16[1536,768]{1,0:T(8,128)(2,1)}), bf16[3072,768]{1,0:T(8,128)(2,1)}) %all-gather.19.cloned.1.call-update) | async-done | bytes 4718608 | tf_op jit(solution)/shard_map/all_gather | solution.py:271
  214.5 25.8 %fusion.51 = (bf16[3072]{0:T(1024)(128)(2,1)S(1)}, bf16[1024,3072]{1,0:T(8,128)(2,1)S(1)}) fusion(f32[1024,3072]{1,0:T(8,128)} %fusion.45, f32[3072]{0:T(1024)S(1)} %bitcast.74, bf16[1024,768]{1,0:T(8,128)(2,1)} %param.27, bf16[3072,768]{1,0:T(8,128)(2,1)} %all-gather.19.cloned.1.call-done), kind=kOutput, calls=%fused_computation.112 | convolution fusion | flops 4897895424 | bytes 25184256 | tf_op jit(solution)/shard_map/dot_general | solution.py:158
  240.4 6.7 fusion.50
  270.7 12.9 %convolution_bitcast_fusion = f32[2,512,1,12,64]{1,4,3,0,2:T(8,128)} fusion(bf16[2,512,12,64]{1,0,3,2:T(2,128)(2,1)} %reshape.100, f32[2,12,512,512]{2,3,1,0:T(8,128)} %get-tuple-element.92, f32[2,12,512]{2,1,0:T(8,128)S(1)} %log_add_fusion, pred[512,512]{0,1:T(8,128)(4,1)S(1)} %iota_compare_fusion), kind=kOutput, calls=%fused_computation.57 | convolution fusion | flops 830472192 | bytes 30195712 | tf_op jit(solution)/shard_map/shqk,sqhd->skhd/dot_general | solution.py:188
  289.7 20.8 %multiply_convert_fusion = bf16[2,12,512,512]{2,3,1,0:T(8,128)(2,1)} fusion(f32[2,12,512,512]{2,3,1,0:T(8,128)} %get-tuple-element.92, f32[2,12,512]{2,1,0:T(8,128)S(1)} %multiply_reduce_fusion, f32[2,12,512]{2,1,0:T(8,128)} %copy-done.17, pred[512,512]{0,1:T(8,128)(4,1)S(1)} %iota_compare_fusion, bf16[2,512,1,12,64]{1,0,4,3,2:T(2,128)(2,1)} %copy-done.15, ...), kind=kOutput, calls=%fused_computation | convolution fusion | flops 849346560 | bytes 41254912 | tf_op jit(solution)/shard_map/sqhd,skhd->shqk/dot_general | solution.py:189
  310.5 9.1 %convolution_bitcast_fusion.1 = f32[2,512,1,12,64]{1,4,3,0,2:T(8,128)S(1)} fusion(bf16[2,12,512,512]{2,3,1,0:T(8,128)(2,1)} %multiply_convert_fusion, bf16[2,512,1,12,64]{1,0,4,3,2:T(2,128)(2,1)} %copy-done.8), kind=kOutput, calls=%fused_computation.58 | convolution fusion | flops 805306368 | bytes 17301504 | tf_op jit(solution)/shard_map/shqk,sqhd->skhd/dot_general | solution.py:194
  328.7 8.0 copy.87
  352.6 12.6 %convolution_convert_fusion = bf16[3072,768]{1,0:T(8,128)(2,1)} fusion(bf16[1024,768]{1,0:T(8,128)(2,1)} %param.27, f32[1024,3072]{1,0:T(8,128)} %fusion.45, f32[3072]{0:T(1024)S(1)} %bitcast.75), kind=kOutput, calls=%fused_computation.17 | convolution fusion | flops 4865654784 | bytes 18886656 | tf_op jit(solution)/shard_map/dot_general | solution.py:156
  365.3 9.8 %convolution_convert_fusion.1 = bf16[768,3072]{1,0:T(8,128)(2,1)} fusion(bf16[1024,3072]{1,0:T(8,128)(2,1)} %copy-done.27, f32[1024,768]{0,1:T(8,128)S(1)} %get-tuple-element.94, f32[768]{0:T(1024)S(1)} %reshape.122, f32[768]{0:T(1024)S(1)} %reshape.121, f32[1024]{0:T(1024)S(1)} %add_rsqrt_fusion, f32[1024]{0:T(1024)S(1)} %broadcast_multiply_fusion.4), kind=kOutput, calls=%fused_computation.18 | convolution fusion | flops 4838129664 | bytes 14170112 | tf_op jit(solution)/shard_map/dot_general | solution.py:168
  384.5 11.7 %add_convert_fusion.1 = bf16[1024,768]{0,1:T(8,128)(2,1)} fusion(f32[1024,768]{0,1:T(8,128)S(1)} %get-tuple-element.94, bf16[3072,768]{1,0:T(8,128)(2,1)} %all-gather.19.cloned.1.call-done, f32[768]{0:T(1024)S(1)} %reshape.124, f32[1024,3072]{1,0:T(8,128)} %fusion.45, f32[3072]{0:T(1024)S(1)} %bitcast.76), kind=kOutput, calls=%fused_computation.48 | convolution fusion | flops 4865654784 | bytes 22035456 | tf_op jit(solution)/shard_map/dot_general | solution.py:92
  398.7 10.3 %fusion.49 = (bf16[768]{0:T(1024)(128)(2,1)S(1)}, f32[1024,768]{1,0:T(8,128)}) fusion(bf16[768,2304]{1,0:T(8,128)(2,1)} %all-gather.13.cloned.1.call-done, f32[1024,2304]{0,1:T(8,128)} %bitcast.68), kind=kOutput, calls=%fused_computation.110 | convolution fusion | flops 3627023616 | bytes 16123392 | tf_op jit(solution)/shard_map/dot_general | solution.py:201
  423.9 7.8 all-reduce.9
  432.3 31.6 %reduce-scatter.11.cloned.1.call-done = bf16[1536,768]{1,0:T(8,128)(2,1)} async-done(((bf16[3072,768]{1,0:T(8,128)(2,1)}), bf16[1536,768]{1,0:T(8,128)(2,1)}) %reduce-scatter.11.cloned.1.call-update) | async-done | bytes 2359312 | tf_op jit(solution)/shard_map/reduce_scatter | solution.py:307
  464.0 63.0 %reduce-scatter.9.cloned.1.call-done = bf16[384,3072]{1,0:T(8,128)(2,1)} async-done(((bf16[768,3072]{1,0:T(8,128)(2,1)}), bf16[384,3072]{1,0:T(8,128)(2,1)}) %reduce-scatter.9.cloned.1.call-update) | async-done | bytes 2359312 | tf_op jit(solution)/shard_map/reduce_scatter | solution.py:301
  526.9 300.4 %all-reduce.11 = (f32[384]{0:T(512)}, f32[384]{0:T(512)}, f32[384,2304]{1,0:T(8,128)}, f32[768]{0:T(1024)}, f32[384,768]{1,0:T(8,128)}, /*index=5*/f32[384]{0:T(...) all-reduce(f32[384]{0:T(512)S(1)} %dynamic-slice_convert_fusion.7, ...), channel_id=1, replica_groups=mesh['rep'=16,'shard'=2] {'rep'}, use_global_device_ids=true, to_apply=%region_12.13 | all-reduce | flops 3543552 | bytes 21270528 | tf_op jit(solution)/shard_map/psum | solution.py:314
  (155 shorter events, 133.3 us)
Async XLA Ops:
  7.2 54.7 %all-gather.13.cloned.1.call-start = ((), (), s32[]{:S(2)}) async-start(), calls=%async_computation.4 | async-start | bytes 5308416 | tf_op jit(solution)/shard_map/all_gather | solution.py:263
  7.9 7.6 copy-start.21
  7.9 12.0 %copy-start.22 = (bf16[384]{0:T(512)(128)(2,1)S(1)}, bf16[384]{0:T(512)(128)(2,1)}, u32[]{:S(2)}) copy-start(bf16[384]{0:T(512)(128)(2,1)} %param.20) | copy-start | bytes 2308
  7.9 16.4 %copy-start.23 = (bf16[384]{0:T(512)(128)(2,1)S(1)}, bf16[384]{0:T(512)(128)(2,1)}, u32[]{:S(2)}) copy-start(bf16[384]{0:T(512)(128)(2,1)} %param.21) | copy-start | bytes 2308
  8.0 21.1 %copy-start.24 = (bf16[384]{0:T(512)(128)(2,1)S(1)}, bf16[384]{0:T(512)(128)(2,1)}, u32[]{:S(2)}) copy-start(bf16[384]{0:T(512)(128)(2,1)} %param.22) | copy-start | bytes 2308
  8.0 25.7 %copy-start.19 = (bf16[768]{0:T(1024)(128)(2,1)S(1)}, bf16[768]{0:T(1024)(128)(2,1)}, u32[]{:S(2)}) copy-start(bf16[768]{0:T(1024)(128)(2,1)} %param.18) | copy-start | bytes 4612
  8.0 30.3 %copy-start.18 = (bf16[1536]{0:T(1024)(128)(2,1)S(1)}, bf16[1536]{0:T(1024)(128)(2,1)}, u32[]{:S(2)}) copy-start(bf16[1536]{0:T(1024)(128)(2,1)} %param.24) | copy-start | bytes 9220
  8.0 121.4 %all-gather.15.cloned.1.call-start = ((), (), s32[]{:S(2)}) async-start(), calls=%async_computation.5 | async-start | bytes 1769472 | tf_op jit(solution)/shard_map/all_gather | solution.py:265
  8.7 141.7 %all-gather.17.cloned.1.call-start = ((), (), s32[]{:S(2)}) async-start(), calls=%async_computation.6 | async-start | bytes 7077888 | tf_op jit(solution)/shard_map/all_gather | solution.py:269
  9.5 205.0 %all-gather.19.cloned.1.call-start = ((), (), s32[]{:S(2)}) async-start(), calls=%async_computation.7 | async-start | bytes 7077888 | tf_op jit(solution)/shard_map/all_gather | solution.py:271
  10.0 422.3 %reduce-scatter.7.cloned.1.call-start = ((), (), s32[]{:S(2)}) async-start(), calls=%async_computation.9 | async-start | bytes 1769472 | tf_op jit(solution)/shard_map/reduce_scatter | solution.py:289
  44.8 17.1 %copy-start = (bf16[1024,768]{0,1:T(8,128)(2,1)}, bf16[1024,768]{0,1:T(8,128)(2,1)S(1)}, u32[]{:S(2)}) copy-start(bf16[1024,768]{0,1:T(8,128)(2,1)S(1)} %copy.70) | copy-start | bytes 4718596
  90.1 12.2 %copy-start.6 = (bf16[2,512,1,12,64]{1,0,4,3,2:T(2,128)(2,1)}, bf16[2,512,1,12,64]{1,0,4,3,2:T(2,128)(2,1)S(1)}, u32[]{:S(2)}) copy-start(bf16[2,512,1,12,64]{1,0,4,3,2:T(2,128)(2,1)S(1)} %get-tuple-element.88) | copy-start | bytes 4718596
  90.1 12.2 %copy-start.8 = (bf16[2,512,1,12,64]{1,0,4,3,2:T(2,128)(2,1)}, bf16[2,512,1,12,64]{1,0,4,3,2:T(2,128)(2,1)S(1)}, u32[]{:S(2)}) copy-start(bf16[2,512,1,12,64]{1,0,4,3,2:T(2,128)(2,1)S(1)} %get-tuple-element.89) | copy-start | bytes 4718596
  90.1 23.3 %copy-start.15 = (bf16[2,512,1,12,64]{1,0,4,3,2:T(2,128)(2,1)}, bf16[2,512,1,12,64]{1,0,4,3,2:T(2,128)(2,1)S(1)}, u32[]{:S(2)}) copy-start(bf16[2,512,1,12,64]{1,0,4,3,2:T(2,128)(2,1)S(1)} %get-tuple-element.90) | copy-start | bytes 4718596
  113.5 157.3 %copy-start.17 = (f32[2,12,512]{2,1,0:T(8,128)}, f32[2,12,512]{2,1,0:T(8,128)S(1)}, u32[]{:S(2)}) copy-start(f32[2,12,512]{2,1,0:T(8,128)S(1)} %log_add_fusion) | copy-start | bytes 147460
  214.5 25.9 %copy-start.14 = (bf16[768,3072]{1,0:T(8,128)(2,1)S(1)}, bf16[768,3072]{1,0:T(8,128)(2,1)}, u32[]{:S(2)}) copy-start(bf16[768,3072]{1,0:T(8,128)(2,1)} %all-gather.17.cloned.1.call-done) | copy-start | bytes 14155780
  240.4 6.8 copy-start.27
  270.7 12.9 %copy-start.12 = (bf16[2,512,12,64]{1,0,3,2:T(2,128)(2,1)S(1)}, bf16[2,512,12,64]{1,0,3,2:T(2,128)(2,1)}, u32[]{:S(2)}) copy-start(bf16[2,512,12,64]{1,0,3,2:T(2,128)(2,1)} %reshape.100) | copy-start | bytes 4718596
  286.6 145.7 %reduce-scatter.5.cloned.1.call-start = ((), (), s32[]{:S(2)}) async-start(), calls=%async_computation.8 | async-start | bytes 5308416 | tf_op jit(solution)/shard_map/reduce_scatter | solution.py:283
  310.5 9.1 %copy-start.7 = (bf16[2,512,1,12,64]{1,0,4,3,2:T(2,128)(2,1)S(1)}, bf16[2,512,1,12,64]{1,0,4,3,2:T(2,128)(2,1)}, u32[]{:S(2)}) copy-start(bf16[2,512,1,12,64]{1,0,4,3,2:T(2,128)(2,1)} %copy-done.6) | copy-start | bytes 4718596
  336.6 9.8 %copy-start.1 = (bf16[1024,768]{0,1:T(8,128)(2,1)S(1)}, bf16[1024,768]{0,1:T(8,128)(2,1)}, u32[]{:S(2)}) copy-start(bf16[1024,768]{0,1:T(8,128)(2,1)} %copy-done) | copy-start | bytes 4718596
  352.5 111.4 %reduce-scatter.11.cloned.1.call-start = ((), (), s32[]{:S(2)}) async-start(), calls=%async_computation.11 | async-start | bytes 7077888 | tf_op jit(solution)/shard_map/reduce_scatter | solution.py:307
  365.2 161.7 %reduce-scatter.9.cloned.1.call-start = ((), (), s32[]{:S(2)}) async-start(), calls=%async_computation.10 | async-start | bytes 7077888 | tf_op jit(solution)/shard_map/reduce_scatter | solution.py:301
  (12 other events, 31.6 us)
Sparse Core Ops, SparseCore 0:
  9.5 52.3 all-gather.12
  63.4 22.7 all-gather.14
  87.8 62.6 all-gather.16
  151.8 62.6 all-gather.18
  286.7 21.8 reduce-scatter.6
  352.7 47.7 reduce-scatter.4
  403.3 60.5 reduce-scatter.10
  466.8 60.0 reduce-scatter.8
where the time goes:
time: 843 us; the launch traced here: 834 us
  blocking collectives  345 us (41%)
  matrix products  186 us (22%)
  waiting for transfers between devices  182 us (22%)
  local copies, waits for them, and re-layouts  67.4 us (8%)
  other arithmetic  37 us (4%)
  between operations  16.8 us (2%)
    psum x1, blocking collectives, per_device(): lax.psum((owned[0], owned[1], owned[2], owned[3], owned[4], owned[5], own...  300 us
    reduce_scatter x1, waiting for transfers between devices, per_device(): lax.psum_scatter(grads[8].astype(jnp.bfloat16), 'shard', scatter_dimensio...  63 us
    all_gather x1, waiting for transfers between devices, per_device(): lax.all_gather(params[10], 'shard', axis=0, tiled=True)  53 us
    reduce_scatter x1, waiting for transfers between devices, per_device(): lax.psum_scatter(grads[10].astype(jnp.bfloat16), 'shard', scatter_dimensi...  31.6 us
    dot_general x1, matrix products, backward(): d_act = jnp.dot(cotangent, wout.T, preferred_element_type=jnp.float32)  25.8 us
    unnamed x71, local copies, waits for them, and re-layouts  23.3 us
    dot_general x1, matrix products, backward(): jnp.einsum('sqhd,skhd->shqk', d_att, value_rows, preferred_element_type=j...  20.8 us
  transfers between devices with their start and end apart: 8, of which 5 were waited for; matrix products, arithmetic and copies ran while one was open for 26% of the time, Pallas kernels for 0%

commit v1 on v0

v1 whole, which is shorter than its diff:
```python
import functools
import types

import jax
import jax.numpy as jnp
from jax import lax
from jax.experimental import pallas as pl
from jax.experimental.pallas import tpu as pltpu
from jax.sharding import PartitionSpec as P

HEAD_DIM = 64
SEQ_LEN = 512
EPS = 1e-05
GELU_C = 0.7978845608028654
F32, BF16 = jnp.float32, jnp.bfloat16
MESH = pl.DeviceIdType.MESH
LANES = 128
BLK = 256
NEG = -1e30
VECS = ("ln1g", "ln1b", "qvb", "projb", "ln2g", "ln2b", "outb", "fcb")


def dims_of(mesh, rows, width, ff):
    d = types.SimpleNamespace()
    d.R, d.S = mesh.shape["rep"], mesh.shape["shard"]
    d.nb = d.R.bit_length() - 1
    assert d.S == 2 and d.R == 1 << d.nb and d.nb >= 4
    d.M, d.D, d.FF = rows, width, ff
    d.DH, d.FH = width // 2, ff // 2
    d.NJ = ff // BLK
    d.NP = width // BLK
    d.NH2 = width // LANES
    d.NSEQ = rows // SEQ_LEN
    d.NCH = 2 * d.NJ + 4 * d.NP
    d.PR = d.DH // 8
    d.PO = LANES // 8
    half = {"qvb": width, "fcb": ff // 2}
    d.off, at = {}, 0
    for name in VECS:
        d.off[name] = (at, half.get(name, width // 2))
        at += d.off[name][1]
    d.NV = at
    d.lag = [2, 3, 3, 2, 2] + [2] * (d.nb - 4) + [2, 2, 3, 2]
    d.NS = 2 * max(d.lag)
    d.first_ag = d.nb + 1
    d.B, d.E, at = [], [], 0
    for i, lag in enumerate(d.lag + [2]):
        at += i == d.first_ag
        d.B.append(at)
        at += lag
        d.E.append(at)
    d.V0 = 2 * d.NJ + d.NP
    d.GU = 2 * d.NSEQ
    d.GV = d.GU + 3
    d.NVS = d.V0 + d.NP * d.GV
    d.NQP = 6
    d.QW = 3 * width // d.NQP
    return d


def scratch_of(d):
    vm, sem = pltpu.VMEM, pltpu.SemaphoreType.DMA
    P8 = (2, d.PR, LANES)
    n_x = d.nb - 4
    items = [
        ("WQ", vm((d.D, 3 * d.D), BF16)),
        ("WP", vm((d.D, d.D), BF16)),
        ("WF", vm((d.NJ, d.D, BLK), BF16)),
        ("WO", vm((d.NJ, BLK, d.D), BF16)),
        ("ACC", vm((d.NCH, 2, 8) + P8, BF16)),
        ("R0", vm((d.NS, 2, 4) + P8, BF16)),
        ("R1", vm((d.NS, 4) + P8, BF16)),
        ("R2", vm((d.NS, 2) + P8, BF16)),
        ("R3", vm((d.NS, 1) + P8, BF16)),
        ("R4", vm((d.NS, d.PR, LANES), BF16)),
        ("RX", vm((max(n_x, 1), d.NS, d.PR, LANES), BF16)),
        ("QKV", vm((d.M, 3 * d.D), BF16)),
        ("T", vm((d.M, d.D), BF16)),
        ("COT", vm((d.M, d.D), BF16)),
        ("N1", vm((d.M, d.D), BF16)),
        ("ATT", vm((d.M, d.D), BF16)),
        ("N2", vm((d.M, d.D), BF16)),
        ("N2T", vm((d.D, d.M), BF16)),
        ("HRES", vm((d.M, d.D), F32)),
        ("OUTACC", vm((d.M, d.D), F32)),
        ("DN2", vm((d.M, d.D), F32)),
        ("ACTT", vm((BLK, d.M), BF16)),
        ("DPRE", vm((d.M, BLK), BF16)),
        ("VA", vm((1, d.NV), F32)),
        ("VB", vm((1, d.NV), F32)),
        ("VX", vm((1, d.NV), F32)),
        ("VG", vm((2, 1, d.NV), F32)),
        ("VR", vm((d.nb + 1, 1, d.NV), F32)),
        ("LS", sem((4 + d.NJ,))),
        ("GS", sem((3, d.NQP + 1 + d.NJ))),
        ("GR", sem((3, d.NQP + 1 + d.NJ))),
        ("SS", sem((len(d.lag), d.NS))),
        ("SR", sem((len(d.lag), d.NS))),
        ("OS", sem((d.NS,))),
        ("CR", pltpu.SemaphoreType.REGULAR((4,))),
        ("VS", sem((d.nb + 2,))),
        ("VQ", sem((d.nb + 2,))),
    ]
    return [n for n, _ in items], [s for _, s in items]


def nt(a, b):
    return lax.dot_general(a, b, (((1,), (1,)), ((), ())), preferred_element_type=F32)


def nn(a, b):
    return jnp.dot(a, b, preferred_element_type=F32)


def tn(a, b):
    return lax.dot_general(a, b, (((0,), (0,)), ((), ())), preferred_element_type=F32)


def norm_rows(v):
    c = v - jnp.mean(v, axis=-1, keepdims=True)
    r = lax.rsqrt(jnp.mean(c * c, axis=-1, keepdims=True) + EPS)
    return c * r, r


def mult(x, m):
    return x if isinstance(x, int) else pl.multiple_of(x, m)


def guarded(cond, fn):
    if isinstance(cond, bool):
        if cond:
            fn()
    else:
        pl.when(cond)(fn)


def both(a, b):
    if isinstance(a, bool):
        return b if a else False
    if isinstance(b, bool):
        return a if b else False
    return jnp.logical_and(a, b)


def block_kernel(d, names, tok, cot, wq, wp, wf, wo, vec, out_o, dx_o, gr_o, vo_o, *scratch):
    k = types.SimpleNamespace(**dict(zip(names, scratch)))
    rep, s = lax.axis_index("rep"), lax.axis_index("shard")
    bit = [lax.rem(lax.div(rep, 1 << i), 2) for i in range(d.nb)]

    def rep_peer(i):
        return {"rep": rep + (1 - 2 * bit[i]) * (1 << i), "shard": s}

    x_peer = {"rep": rep, "shard": 1 - s}
    b0, b1, b2, b3 = bit[:4]
    o = 1 - s

    barrier = pltpu.get_barrier_semaphore()
    peers = [x_peer] + [rep_peer(i) for i in range(d.nb)]
    for peer in peers:
        pl.semaphore_signal(barrier, inc=1, device_id=peer, device_id_type=MESH)
    pl.semaphore_wait(barrier, len(peers))

    def remote(src, dst, ss, rs, peer):
        return pltpu.make_async_remote_copy(
            src_ref=src, dst_ref=dst, send_sem=ss, recv_sem=rs, device_id=peer, device_id_type=MESH
        )

    g = b0 * 2 + b1
    QR, OR = d.DH // 4, LANES // 4
    NQP, NG = d.NQP, d.NQP + 1 + d.NJ
    vcopy = remote(vec, k.VX, k.VS.at[d.nb + 1], k.VQ.at[d.nb + 1], x_peer)
    vcopy.start()
    tcopy = pltpu.make_async_copy(tok, k.T, k.LS.at[0])
    tcopy.start()

    def gather_copies(hop, p):
        if isinstance(p, int) and p <= NQP:
            ref, src = (k.WQ, wq) if p < NQP else (k.WP, wp)
            cols = pl.ds(p * d.QW, d.QW) if p < NQP else pl.ds(0, d.D)
            if hop == 0:
                return [(src.at[pl.ds(g * QR, QR), cols], ref.at[pl.ds(s * d.DH + g * QR, QR), cols])]
            if hop == 1:
                at = ref.at[pl.ds(o * d.DH + g * QR, QR), cols]
            else:
                at = ref.at[pl.ds(o * d.DH + b0 * 2 * QR, 2 * QR), cols]
            return [(at, at)]
        j = p - NQP - 1
        if hop == 0:
            pairs = []
            for strip in range(2):
                col = mult(strip * d.FH + j * LANES, LANES)
                pairs.append((
                    wf.at[pl.ds(g * QR, QR), pl.ds(col, LANES)],
                    k.WF.at[j, pl.ds(s * d.DH + g * QR, QR), pl.ds(strip * LANES, LANES)],
                ))
            pairs.append((
                wo.at[pl.ds(mult(j * LANES + g * OR, OR), OR), :],
                k.WO.at[j, pl.ds(s * LANES + g * OR, OR), :],
            ))
            return pairs
        if hop == 1:
            fa = k.WF.at[j, pl.ds(o * d.DH + g * QR, QR), :]
            oa = k.WO.at[j, pl.ds(o * LANES + g * OR, OR), :]
        else:
            fa = k.WF.at[j, pl.ds(o * d.DH + b0 * 2 * QR, 2 * QR), :]
            oa = k.WO.at[j, pl.ds(o * LANES + b0 * 2 * OR, 2 * OR), :]
        return [(fa, fa), (oa, oa)]

    hop_peer = [x_peer, rep_peer(1), rep_peer(0)]

    def g_start(hop, p):
        for a, b in gather_copies(hop, p):
            remote(a, b, k.GS.at[hop, p], k.GR.at[hop, p], hop_peer[hop]).start()

    def g_wait(hop, p):
        if isinstance(p, int) and p <= NQP:
            (a, b), = gather_copies(hop, p)
            remote(a, b, k.GS.at[hop, p], k.GR.at[hop, p], hop_peer[hop]).wait()
        else:
            rows = k.WF.at[0, pl.ds(0, d.D // 4 * (2 if hop == 2 else 1)), :]
            pltpu.make_async_copy(rows, rows, k.GS.at[hop, p]).wait()
            pltpu.make_async_copy(rows, rows, k.GR.at[hop, p]).wait()

    own_q = pltpu.make_async_copy(wq, k.WQ.at[pl.ds(s * d.DH, d.DH), :], k.LS.at[1])
    own_q.start()
    for p in range(NQP + 1):
        g_start(0, p)

    def start_blocks(j, _):
        g_start(0, j + NQP + 1)
        return 0

    lax.fori_loop(0, d.NJ, start_blocks, 0)
    own_p = pltpu.make_async_copy(wp, k.WP.at[pl.ds(s * d.DH, d.DH), :], k.LS.at[2])
    own_p.start()
    ccopy = pltpu.make_async_copy(cot, k.COT, k.LS.at[3])
    ccopy.start()

    def start_own(j, _):
        for strip in range(2):
            pltpu.make_async_copy(
                wf.at[:, pl.ds(mult(strip * d.FH + j * LANES, LANES), LANES)],
                k.WF.at[j, pl.ds(s * d.DH, d.DH), pl.ds(strip * LANES, LANES)],
                k.LS.at[4 + j],
            ).start()
        pltpu.make_async_copy(
            wo.at[pl.ds(mult(j * LANES, LANES), LANES), :],
            k.WO.at[j, pl.ds(s * LANES, LANES), :],
            k.LS.at[4 + j],
        ).start()
        return 0

    lax.fori_loop(0, d.NJ, start_own, 0)

    def wait_own(j):
        pltpu.make_async_copy(k.WF.at[0], k.WF.at[0], k.LS.at[4 + j]).wait()

    vcopy.wait()
    own, oth = vec[...], k.VX[...]
    first = s == 0
    k.VA[...] = jnp.where(first, own, oth)
    k.VB[...] = jnp.where(first, oth, own)

    def full(name):
        at, n = d.off[name]
        return jnp.concatenate([k.VA[:, at:at + n], k.VB[:, at:at + n]], axis=1)

    def put_vec(name, value):
        at, n = d.off[name]
        k.VG[0, :, at:at + n] = value[:, :n]
        k.VG[1, :, at:at + n] = value[:, n:]

    tcopy.wait()
    LR = 64

    def norm1(i, _):
        rows = pl.ds(pl.multiple_of(i * LR, LR), LR)
        xhat, _r = norm_rows(k.T[rows, :].astype(F32))
        k.N1[rows, :] = (xhat * full("ln1g") + full("ln1b")).astype(BF16)
        return 0

    lax.fori_loop(0, d.M // LR, norm1, 0)
    own_q.wait()
    for p in range(NQP + 2):
        for hop in range(2, -1, -1):
            if 0 <= p - hop < NQP:
                g_wait(hop, p - hop)
                if hop < 2:
                    g_start(hop + 1, p - hop)

    bq = k.VA[:, d.off["qvb"][0]:d.off["qvb"][0] + d.D]
    bv = k.VB[:, d.off["qvb"][0]:d.off["qvb"][0] + d.D]
    RB = 256

    def qkv_rows(i, _):
        rows = pl.ds(pl.multiple_of(i * RB, RB), RB)
        x = k.N1[rows, :]
        for part in range(3):
            y = nn(x, k.WQ[:, part * d.D:(part + 1) * d.D])
            if part == 0:
                y = (y + bq).astype(BF16) * jnp.asarray(HEAD_DIM ** -0.5, BF16)
            elif part == 1:
                y = y.astype(BF16)
            else:
                y = (y + bv).astype(BF16)
            k.QKV[rows, part * d.D:(part + 1) * d.D] = y
        return 0

    lax.fori_loop(0, d.M // RB, qkv_rows, 0)

    lane = lax.broadcasted_iota(jnp.int32, (1, LANES), 1)
    head_mask = [lane < HEAD_DIM, lane >= HEAD_DIM]
    zero = jnp.zeros((), BF16)
    QB = 256
    NQB = SEQ_LEN // QB
    tri = lax.broadcasted_iota(jnp.int32, (QB, QB), 1) <= lax.broadcasted_iota(jnp.int32, (QB, QB), 0)
    tri_t = lax.broadcasted_iota(jnp.int32, (QB, QB), 0) <= lax.broadcasted_iota(jnp.int32, (QB, QB), 1)

    def unit_refs(seq, hp):
        rows = pl.ds(pl.multiple_of(seq * SEQ_LEN, SEQ_LEN), SEQ_LEN)
        cols = [pl.ds(pl.multiple_of(part * d.D + hp * LANES, LANES), LANES) for part in range(3)]
        return rows, cols

    g_wait(0, NQP)
    g_start(1, NQP)
    g_wait(1, NQP)
    g_start(2, NQP)
    g_wait(2, NQP)

    def attend_loop(u, _):
        attend_body(u)
        return 0

    def g_block_tick(p):
        for hop in range(2, -1, -1):
            q = p - hop

            def do(hop=hop, q=q):
                g_wait(hop, q)
                if hop < 2:
                    g_start(hop + 1, q)

            guarded(jnp.logical_and(q > NQP, q < NG), do)

    def attend_body(u):
        seq, hp = lax.div(u, d.NH2), lax.rem(u, d.NH2)
        rows, cols = unit_refs(seq, hp)
        q2, k2, v2 = (k.QKV[rows, c] for c in cols)
        for i in range(NQB):
            klen = (i + 1) * QB
            total = None
            for mask in head_mask:
                qm = jnp.where(mask, q2[i * QB:klen], zero)
                vm = jnp.where(mask, v2[:klen], zero)
                sc = nt(qm, k2[:klen])
                diag = jnp.where(tri, sc[:, klen - QB:], NEG)
                sc = diag if i == 0 else jnp.concatenate([sc[:, :klen - QB], diag], axis=1)
                top = jnp.max(sc, axis=1, keepdims=True)
                e = jnp.exp(sc - top)
                den = jnp.sum(e, axis=1, keepdims=True)
                part = nn(e.astype(BF16), vm) * (1.0 / den)
                total = part if total is None else total + part
            out_rows = pl.ds(pl.multiple_of(seq * SEQ_LEN + i * QB, QB), QB)
            k.ATT[out_rows, pl.ds(pl.multiple_of(hp * LANES, LANES), LANES)] = total.astype(BF16)
        g_block_tick(u + NQP + 1)

    lax.fori_loop(0, d.NSEQ * d.NH2, attend_loop, 0)
    own_p.wait()

    HB = 128

    def hres_rows(i, _):
        rows = pl.ds(pl.multiple_of(i * HB, HB), HB)
        h = k.T[rows, :].astype(F32) + nn(k.ATT[rows, :], k.WP[...]) + full("projb")
        k.HRES[rows, :] = h
        k.OUTACC[rows, :] = h + full("outb")
        xhat, _r = norm_rows(h)
        n2 = (xhat * full("ln2g") + full("ln2b")).astype(BF16)
        k.N2[rows, :] = n2
        k.N2T[:, rows] = n2.T
        k.DN2[rows, :] = jnp.zeros((HB, d.D), F32)
        return 0

    lax.fori_loop(0, d.M // HB, hres_rows, 0)
    ccopy.wait()

    def cot_sum(i, total):
        rows = pl.ds(pl.multiple_of(i * LR, LR), LR)
        return total + jnp.sum(k.COT[rows, :].astype(F32), axis=0, keepdims=True)

    put_vec("outb", lax.fori_loop(0, d.M // LR, cot_sum, jnp.zeros((1, d.D), F32)))

    lo4, lo2 = 4 * b0, 4 * b0 + 2 * b1
    lo1 = lo2 + b2
    n_x = d.nb - 4
    last = len(d.lag)

    def stage(i, c):
        slot = lax.rem(c, d.NS)
        sems = (k.SS.at[i, slot], k.SR.at[i, slot])
        A = k.ACC
        if i == 0:
            return A.at[c, :, pl.ds(4 - lo4, 4)], k.R0.at[slot], sems, rep_peer(0), (A.at[c, :, pl.ds(lo4, 4)], k.R0.at[slot])
        if i == 1:
            return A.at[c, o, pl.ds(lo4, 4)], k.R1.at[slot], sems, x_peer, (A.at[c, s, pl.ds(lo4, 4)], k.R1.at[slot])
        if i == 2:
            return (A.at[c, s, pl.ds(lo4 + 2 - 2 * b1, 2)], k.R2.at[slot], sems, rep_peer(1),
                    (A.at[c, s, pl.ds(lo2, 2)], k.R2.at[slot]))
        if i == 3:
            return (A.at[c, s, pl.ds(lo2 + 1 - b2, 1)], k.R3.at[slot], sems, rep_peer(2),
                    (A.at[c, s, pl.ds(lo1, 1)], k.R3.at[slot]))
        if i == 4:
            return A.at[c, s, lo1, 1 - b3], k.R4.at[slot], sems, rep_peer(3), (A.at[c, s, lo1, b3], k.R4.at[slot])
        if i < 5 + n_x:
            dst = k.RX.at[i - 5, slot]
            return A.at[c, s, lo1, b3], dst, sems, rep_peer(i - 1), (A.at[c, s, lo1, b3], dst)
        at = [A.at[c, s, lo1, b3], A.at[c, s, pl.ds(lo1, 1)], A.at[c, s, pl.ds(lo2, 2)], A.at[c, s, pl.ds(lo4, 4)]][i - 5 - n_x]
        return at, at, sems, rep_peer(3 - (i - 5 - n_x)), None

    def chunk_of(v):
        w = v - d.V0
        if isinstance(v, int):
            if v < d.V0:
                return v, 0 <= v
            grp, r = divmod(w, d.GV)
            return d.V0 + 3 * grp + r - d.GU, v < d.NVS and r >= d.GU
        late = v >= d.V0
        w = jnp.maximum(w, 0)
        grp, r = lax.div(w, d.GV), lax.rem(w, d.GV)
        c = jnp.where(late, d.V0 + 3 * grp + r - d.GU, v)
        ok = jnp.logical_and(v >= 0, jnp.logical_and(v < d.NVS, jnp.logical_or(v < d.V0, r >= d.GU)))
        return c, ok

    def out_copy(c):
        return pltpu.make_async_copy(k.ACC.at[c, s], gr_o.at[c], k.OS.at[lax.rem(c, d.NS)])

    def begin(i, c):
        if i == last:
            out_copy(c).start()
            return
        src, dst, (ss, rs), peer, _ = stage(i, c)
        if i >= d.first_ag:
            pl.semaphore_wait(k.CR.at[i - d.first_ag], 1)
        remote(src, dst, ss, rs, peer).start()

    def finish(i, c):
        if i == last:
            out_copy(c).wait()
            return
        src, dst, (ss, rs), peer, add = stage(i, c)
        remote(src, dst, ss, rs, peer).wait()
        if add is not None:
            add[0][...] = add[0][...] + add[1][...]
        if i in credit_of:
            pl.semaphore_signal(k.CR.at[credit_of[i]], inc=1, device_id=peer, device_id_type=MESH)

    credit_of = {4: 0, 3: 1, 2: 2, 0: 3}

    def tick(t):
        for i in range(last, -1, -1):
            c, ok = chunk_of(t - d.E[i])
            guarded(ok, functools.partial(finish, i, c))
        for i in range(last, -1, -1):
            c, ok = chunk_of(t - d.B[i])
            guarded(ok, functools.partial(begin, i, c))

    def put_cols(c, sh, value):
        value = value.astype(BF16)
        for p in range(8):
            for z in range(2):
                k.ACC[c, sh, p, z, :, :] = value[p * d.PR:(p + 1) * d.PR, z * LANES:(z + 1) * LANES]

    def put_out(c, n, value):
        value = value.astype(BF16)
        per = d.D // LANES // 2
        for sh in range(2):
            for p in range(8):
                for h in range(BLK // LANES):
                    t = n * (BLK // LANES) + h
                    k.ACC[c, sh, p, t // per, pl.ds((t % per) * d.PO, d.PO), :] = value[
                        sh * LANES + p * d.PO:sh * LANES + (p + 1) * d.PO, h * LANES:(h + 1) * LANES
                    ]

    f_at = d.off["fcb"][0]
    C1, C3 = GELU_C, GELU_C * 0.044715
    S1, S3 = 2.0 * GELU_C, 2.0 * GELU_C * 0.134145

    def mlp(j, _):
        wait_own(j)
        fcb = jnp.concatenate(
            [v[:, pl.ds(pl.multiple_of(f_at + j * LANES, LANES), LANES)] for v in (k.VA, k.VB)], axis=1
        )

        def rows_step(i, total):
            rows = pl.ds(pl.multiple_of(i * RB, RB), RB)
            wfj, woj = k.WF[j], k.WO[j]
            c = k.COT[rows, :]
            pre = nn(k.N2[rows, :], wfj) + fcb
            d_act = nt(c, woj)
            sq = pre * pre
            h = 0.5 + 0.5 * jnp.tanh(pre * (C1 + C3 * sq))
            a = pre * h
            slope = h + a * (1.0 - h) * (S1 + S3 * sq)
            d_pre = d_act * slope
            ab, db = a.astype(BF16), d_pre.astype(BF16)
            k.ACTT[:, rows] = ab.T
            k.DPRE[rows, :] = db
            k.OUTACC[rows, :] += nn(ab, woj)
            k.DN2[rows, :] += nt(db, wfj)
            return total + jnp.sum(d_pre, axis=0, keepdims=True)

        total = lax.fori_loop(0, d.M // RB, rows_step, jnp.zeros((1, BLK), F32))
        at = pl.ds(pl.multiple_of(f_at + j * LANES, LANES), LANES)
        k.VG[0, :, at] = total[:, :LANES]
        k.VG[1, :, at] = total[:, LANES:]
        for n in range(d.NP):
            put_out(2 * j, n, nn(k.ACTT[...], k.COT[:, n * BLK:(n + 1) * BLK]))
        tick(2 * j)
        for sh in range(2):
            put_cols(2 * j + 1, sh, nn(k.N2T[sh * d.DH:(sh + 1) * d.DH, :], k.DPRE[...]))
        tick(2 * j + 1)
        return 0

    g_wait(1, NG - 1)
    g_start(2, NG - 1)
    g_wait(2, NG - 2)
    g_wait(2, NG - 1)
    lax.fori_loop(0, d.NJ, mlp, 0)

    g2 = full("ln2g")

    def norm2_back(i, sums):
        rows = pl.ds(pl.multiple_of(i * LR, LR), LR)
        k.N1[rows, :] = k.OUTACC[rows, :].astype(BF16)
        xhat, r = norm_rows(k.HRES[rows, :])
        dn = k.DN2[rows, :]
        gg = dn * g2
        dh = k.COT[rows, :].astype(F32) + r * (
            gg - jnp.mean(gg, axis=-1, keepdims=True) - xhat * jnp.mean(gg * xhat, axis=-1, keepdims=True)
        )
        k.DN2[rows, :] = dh
        k.N2[rows, :] = dh.astype(BF16)
        add = lambda v: jnp.sum(v, axis=0, keepdims=True)
        return sums[0] + add(dn * xhat), sums[1] + add(dn), sums[2] + add(dh)

    zrow = jnp.zeros((1, d.D), F32)
    sums = lax.fori_loop(0, d.M // LR, norm2_back, (zrow, zrow, zrow))
    put_vec("ln2g", sums[0])
    put_vec("ln2b", sums[1])
    put_vec("projb", sums[2])
    bcopy = pltpu.make_async_copy(k.N1, out_o, k.LS.at[0])
    bcopy.start()

    def transpose_att(i, _):
        rows = pl.ds(pl.multiple_of(i * HB, HB), HB)
        k.N2T[:, rows] = k.ATT[rows, :].T
        return 0

    lax.fori_loop(0, d.M // HB, transpose_att, 0)

    def proj_cols(n, _):
        c = 2 * d.NJ + n
        cols = pl.ds(pl.multiple_of(n * BLK, BLK), BLK)
        for sh in range(2):
            put_cols(c, sh, nn(k.N2T[sh * d.DH:(sh + 1) * d.DH, :], k.N2[:, cols]))
        tick(c)
        return 0

    lax.fori_loop(0, d.NP, proj_cols, 0)
    bcopy.wait()

    def att_rows(i, _):
        rows = pl.ds(pl.multiple_of(i * RB, RB), RB)
        k.N1[rows, :] = nt(k.N2[rows, :], k.WP[...]).astype(BF16)
        return 0

    lax.fori_loop(0, d.M // RB, att_rows, 0)

    g1, be1 = full("ln1g"), full("ln1b")

    def transpose_n1(i, _):
        rows = pl.ds(pl.multiple_of(i * HB, HB), HB)
        xhat, _r = norm_rows(k.T[rows, :].astype(F32))
        k.N2T[:, rows] = (xhat * g1 + be1).astype(BF16).T
        return 0

    lax.fori_loop(0, d.M // HB, transpose_n1, 0)

    def attend_back(seq, hp):
        rows, cols = unit_refs(seq, hp)
        q2, k2, v2 = (k.QKV[rows, c] for c in cols)
        do2 = k.N1[rows, pl.ds(pl.multiple_of(hp * LANES, LANES), LANES)]
        dq = [None] * NQB
        dk = [None] * NQB
        dv = [None] * NQB

        def acc(lst, n, value):
            lst[n] = value if lst[n] is None else lst[n] + value

        for mask in head_mask:
            km = jnp.where(mask, k2, zero)
            for i in range(NQB):
                klen = (i + 1) * QB
                qm = jnp.where(mask, q2[i * QB:klen], zero)
                dom = jnp.where(mask, do2[i * QB:klen], zero)
                sc = nt(k2[:klen], qm)
                diag = jnp.where(tri_t, sc[klen - QB:], NEG)
                sc = diag if i == 0 else jnp.concatenate([sc[:klen - QB], diag], axis=0)
                top = jnp.max(sc, axis=0, keepdims=True)
                e = jnp.exp(sc - top)
                pr = e * (1.0 / jnp.sum(e, axis=0, keepdims=True))
                dp = nt(v2[:klen], dom)
                delta = jnp.sum(pr * dp, axis=0, keepdims=True)
                ds = (pr * (dp - delta)).astype(BF16)
                dvi = nn(pr.astype(BF16), dom)
                dki = nn(ds, qm)
                for n in range(i + 1):
                    acc(dv, n, dvi[n * QB:(n + 1) * QB])
                    acc(dk, n, dki[n * QB:(n + 1) * QB])
                acc(dq, i, tn(ds, km[:klen]))
        sq = sv = None
        for n in range(NQB):
            r = pl.ds(pl.multiple_of(seq * SEQ_LEN + n * QB, QB), QB)
            dqn = dq[n] * (HEAD_DIM ** -0.5)
            k.QKV[r, cols[0]] = dqn.astype(BF16)
            k.QKV[r, cols[1]] = dk[n].astype(BF16)
            k.QKV[r, cols[2]] = dv[n].astype(BF16)
            a, b = jnp.sum(dqn, axis=0, keepdims=True), jnp.sum(dv[n], axis=0, keepdims=True)
            sq, sv = (a, b) if sq is None else (sq + a, sv + b)
        at = pl.ds(pl.multiple_of(d.off["qvb"][0] + hp * LANES, LANES), LANES)
        for half, value in ((0, sq), (1, sv)):
            k.VG[half, :, at] = k.VG[half, :, at] + value

    for half in range(2):
        at, n = d.off["qvb"]
        k.VG[half, :, at:at + n] = jnp.zeros((1, n), F32)

    def zero_dn1(i, _):
        rows = pl.ds(pl.multiple_of(i * LR, LR), LR)
        k.OUTACC[rows, :] = jnp.zeros((LR, d.D), F32)
        return 0

    lax.fori_loop(0, d.M // LR, zero_dn1, 0)

    def group(grp, _):
        v0 = d.V0 + grp * d.GV

        def unit(u, _):
            attend_back(lax.div(u, 2), 2 * grp + lax.rem(u, 2))
            tick(v0 + u)
            return 0

        lax.fori_loop(0, d.GU, unit, 0)

        def part_step(part, _):
            c = d.V0 + 3 * grp + part
            cols = pl.ds(pl.multiple_of(part * d.D + grp * BLK, BLK), BLK)
            for sh in range(2):
                put_cols(c, sh, nn(k.N2T[sh * d.DH:(sh + 1) * d.DH, :], k.QKV[:, cols]))

            def rows_step(i, _):
                rows = pl.ds(pl.multiple_of(i * RB, RB), RB)
                k.OUTACC[rows, :] += nt(k.QKV[rows, cols], k.WQ[:, cols])
                return 0

            lax.fori_loop(0, d.M // RB, rows_step, 0)
            tick(v0 + d.GU + part)
            return 0

        lax.fori_loop(0, 3, part_step, 0)
        return 0

    lax.fori_loop(0, d.NP, group, 0)

    def norm1_back(i, sums):
        rows = pl.ds(pl.multiple_of(i * LR, LR), LR)
        xhat, r = norm_rows(k.T[rows, :].astype(F32))
        dn = k.OUTACC[rows, :]
        gg = dn * g1
        dx = k.DN2[rows, :] + r * (
            gg - jnp.mean(gg, axis=-1, keepdims=True) - xhat * jnp.mean(gg * xhat, axis=-1, keepdims=True)
        )
        k.COT[rows, :] = dx.astype(BF16)
        add = lambda v: jnp.sum(v, axis=0, keepdims=True)
        return sums[0] + add(dn * xhat), sums[1] + add(dn)

    sums = lax.fori_loop(0, d.M // LR, norm1_back, (zrow, zrow))
    put_vec("ln1g", sums[0])
    put_vec("ln1b", sums[1])
    xcopy = pltpu.make_async_copy(k.COT, dx_o, k.LS.at[0])
    xcopy.start()

    def vec_copy(i):
        src = k.VG.at[o] if i == 0 else k.VG.at[s]
        peer = x_peer if i == 0 else rep_peer(i - 1)
        return remote(src, k.VR.at[i], k.VS.at[i], k.VQ.at[i], peer)

    end = d.NVS + d.E[-1]
    n_v = d.nb + 1
    vec_copy(0).start()
    step = 0
    for t in range(d.NVS, end):
        tick(t)
        if step < n_v and (t - d.NVS) % 2 == 1:
            vec_copy(step).wait()
            k.VG[s] = k.VG[s] + k.VR[step]
            step += 1
            if step < n_v:
                vec_copy(step).start()
    assert step == n_v
    vo_o[...] = k.VG[s]
    xcopy.wait()


def per_device(d, tok, g1, be1, wq, qvb, wp, pb, g2, be2, wf, fb, wo, ob, cot):
    names, scratch = scratch_of(d)
    vec = jnp.concatenate([v.astype(F32) for v in (g1, be1, qvb, pb, g2, be2, ob, fb)]).reshape(1, d.NV)
    hbm = pl.BlockSpec(memory_space=pl.ANY)
    vmem = pl.BlockSpec(memory_space=pltpu.VMEM)
    out, dx, gr, vo = pl.pallas_call(
        functools.partial(block_kernel, d, names),
        out_shape=(
            jax.ShapeDtypeStruct((d.M, d.D), BF16),
            jax.ShapeDtypeStruct((d.M, d.D), BF16),
            jax.ShapeDtypeStruct((d.NCH, 8, 2, d.PR, LANES), BF16),
            jax.ShapeDtypeStruct((1, d.NV), F32),
        ),
        in_specs=[hbm] * 6 + [vmem],
        out_specs=(hbm, hbm, hbm, vmem),
        scratch_shapes=scratch,
        compiler_params=pltpu.CompilerParams(
            collective_id=0, has_side_effects=True, vmem_limit_bytes=67_043_328
        ),
        name="block",
    )(tok, cot, wq, wp, wf, wo, vec)
    vo = vo.reshape(d.NV)
    v = {n: vo[at:at + size] for n, (at, size) in d.off.items()}
    NJ, NP, PR, PO = d.NJ, d.NP, d.PR, d.PO
    mlp = gr[:2 * NJ].reshape(NJ, 2, 8, 2, PR, LANES)
    g_out = mlp[:, 0].reshape(NJ, 8, 2, PR // PO, PO, LANES).transpose(0, 1, 4, 2, 3, 5).reshape(d.FH, d.D)
    g_fc = mlp[:, 1].transpose(1, 3, 2, 0, 4).reshape(d.DH, d.FF)
    g_p = gr[2 * NJ:d.V0].transpose(1, 3, 0, 2, 4).reshape(d.DH, d.D)
    g_q = gr[d.V0:].reshape(NP, 3, 8, 2, PR, LANES).transpose(2, 4, 1, 0, 3, 5).reshape(d.DH, 3 * d.D)
    return (
        out, dx, v["ln1g"], v["ln1b"], g_q.astype(F32), v["qvb"], g_p.astype(F32), v["projb"],
        v["ln2g"], v["ln2b"], g_fc.astype(F32), v["fcb"], g_out.astype(F32), v["outb"],
    )


def solution(mesh):
    def whole(tok, *rest):
        d = dims_of(mesh, tok.shape[0] // (mesh.shape["rep"] * mesh.shape["shard"]), tok.shape[1], rest[9].shape[0])
        both_axes, one, two = P(("rep", "shard"), None), P("shard"), P("shard", None)
        in_specs = (both_axes, one, one, two, one, two, one, one, one, two, one, two, one, both_axes)
        out_specs = (both_axes, both_axes, one, one, two, one, two, one, one, one, two, one, two, one)
        return jax.shard_map(
            functools.partial(per_device, d), mesh=mesh, in_specs=in_specs, out_specs=out_specs, check_vma=False
        )(tok, *rest)

    return whole
```

time: 843 us -> 323 us (0.38)
  blocking collectives: 345 us -> 0 us
  Pallas kernels: 0 us -> 262 us
  matrix products: 186 us -> 0 us
  waiting for transfers between devices: 182 us -> 0 us
  other arithmetic: 37 us -> 8.07 us
  between operations: 16.8 us -> 0.72 us
  local copies, waits for them, and re-layouts: 67.4 us -> 51.4 us
    psum x1 -> x0, blocking collectives: 300 us -> none  [per_device(): lax.psum((owned[0], owned[1], owned[2], owned[3], owned[4], owned[5], own...]
    pallas_call x0 -> x1, Pallas kernels: none -> 262 us  [per_device(): pl.pallas_call(functools.partial(block_kernel, d, names), out_shape=(jax....]
    dot_general x18 -> x0, matrix products: 186 us -> none  [the longest x1 25.8 us: backward(): d_act = jnp.dot(cotangent, wout.T, preferred_element_type=jnp.float32)]
    reduce_scatter x4 -> x0, waiting for transfers between devices: 94.6 us -> none  [the longest x1 63 us: per_device(): lax.psum_scatter(grads[8].astype(jnp.bfloat16), 'shard', scatter_dimensio...]
    all_gather x4 -> x0, waiting for transfers between devices: 84.5 us -> none  [the longest x1 53 us: per_device(): lax.all_gather(params[10], 'shard', axis=0, tiled=True)]
    all_gather x8 -> x0, blocking collectives: 36.9 us -> none  [the longest x1 5.28 us: per_device(): lax.all_gather(params[0], 'shard', axis=0, tiled=True)]
    reduce_sum x9 -> x0, other arithmetic: 24.6 us -> none  [the longest x1 11.1 us: forward(): jnp.sum(jnp.exp(scores - top), axis=-1, keepdims=True)]
    convert_element_type x9 -> x7, local copies, waits for them, and re-layouts: 11 us -> 29.2 us  [the longest x2 14 us: per_device(): g_out.astype(F32)]
  transfers between devices with their start and end apart: 8 -> 0, of which waited for: 5 -> 0; matrix products, arithmetic and copies ran while one was open for 26% -> 0% of each run, Pallas kernels for 0% -> 0%
where the time goes in v1:
time: 323 us; the launch traced here: 322 us
  Pallas kernels  262 us (81%)
  local copies, waits for them, and re-layouts  51.4 us (16%)
  other arithmetic  8.07 us (2%)
    pallas_call x1, Pallas kernels, per_device(): pl.pallas_call(functools.partial(block_kernel, d, names), out_shape=(jax....  262 us
    convert_element_type x2, local copies, waits for them, and re-layouts, per_device(): g_out.astype(F32)  14 us
    unnamed x15, local copies, waits for them, and re-layouts  9.14 us
    convert_element_type x1, local copies, waits for them, and re-layouts, per_device(): g_fc.astype(F32)  6.86 us

profile of v1, /device:TPU:0, one launch (start us, length us, event | category | flops | bytes accessed | tf_op | source)
XLA Modules:
  0.0 322.3 jit_solution(3616465196213266250)
XLA Ops:
  0.7 0.9 dynamic-update-slice
  1.5 0.9 dynamic-update-slice.1
  3.2 0.9 dynamic-update-slice.3
  4.1 0.9 dynamic-update-slice.4
  5.0 0.9 dynamic-update-slice.5
  5.8 0.9 dynamic-update-slice.6
  8.0 262.1 %block.1 = (bf16[1024,768]{1,0:T(8,128)(2,1)}, bf16[1024,768]{1,0:T(8,128)(2,1)}, bf16[36,8,2,48,128]{4,3,2,1,0:T(8,128)(2,1)}, f32[1,4608]{1,0:T(1,128)}) custom-call(bf16[1024,768]{1,0:T(8,128)(2,1)} %tok.1, bf16[1024,768]{1,0:T(8,128)(2,1)} %cot.1, bf16[384,2304]{1,0:T(8,128)(2,1)} %wq.1, bf16[384,768]{1,0:T(8,128)(2,1)} %wp.1, bf16[384,3072]{1,0:T(8,128)(2,1)} %wf.1, ...), custom_call_target="tpu_custom_call" | custom-call | tf_op jit(solution)/shard_map/block/pallas_call | solution.py:720
  270.1 1.3 slice_reduce_fusion.1
  271.3 1.3 slice_reduce_fusion
  272.7 1.3 slice_reduce_fusion.2
  274.0 1.2 convert_bitcast_fusion.3
  275.8 2.0 reshape.70
  277.7 1.8 slice.67
  279.5 3.1 slice.77
  282.7 3.0 fusion
  286.1 1.8 copy.34
  288.0 3.9 %reshape.69 = f32[384,2304]{1,0:T(8,128)} reshape(f32[8,48,3,3,2,128]{5,4,3,2,1,0:T(2,128)S(1)} %copy.34) | data formatting | bytes 7077888 | tf_op jit(solution)/shard_map/convert_element_type | solution.py:745
  291.9 2.3 convert_bitcast_fusion.1
  294.2 5.6 %copy.38 = f32[12,8,16,2,3,128]{5,4,3,2,1,0:T(4,128)} copy(f32[12,8,16,2,3,128]{5,2,4,3,1,0:T(8,128)S(1)} %convert_bitcast_fusion.1) | data formatting | bytes 9437184 | tf_op jit(solution)/shard_map/convert_element_type | solution.py:746
  299.9 8.3 %reshape.72 = f32[1536,768]{1,0:T(8,128)} reshape(f32[12,8,16,2,3,128]{5,4,3,2,1,0:T(4,128)} %copy.38) | data formatting | bytes 9437184 | tf_op jit(solution)/shard_map/convert_element_type | solution.py:746
  308.2 4.1 %convert_bitcast_fusion = f32[8,48,2,12,128]{4,3,2,1,0:T(8,128)} fusion(bf16[12,1,8,2,48,128]{5,4,3,2,1,0:T(8,128)(2,1)S(1)} %copy-done), kind=kLoop, calls=%fused_computation | loop fusion | flops 1179648 | bytes 7077888 | tf_op jit(solution)/shard_map/convert_element_type | solution.py:746
  312.3 6.9 %reshape.71 = f32[384,3072]{1,0:T(8,128)} reshape(f32[8,48,2,12,128]{4,3,2,1,0:T(8,128)} %convert_bitcast_fusion) | data formatting | bytes 9437184 | tf_op jit(solution)/shard_map/convert_element_type | solution.py:746
  319.2 1.1 copy.54
  321.2 1.1 copy.55
  (12 shorter events, 4.1 us)
Async XLA Ops:
  299.9 8.3 %copy-start = (bf16[12,1,8,2,48,128]{5,4,3,2,1,0:T(8,128)(2,1)S(1)}, bf16[12,1,8,2,48,128]{5,4,3,2,1,0:T(8,128)(2,1)}, u32[]{:S(2)}) copy-start(bf16[12,1,8,2,48,128]{5,4,3,2,1,0:T(8,128)(2,1)} %get-tuple-element.29) | copy-start | bytes 7077892
  312.3 6.9 %copy-start.2 = (bf16[1024,768]{1,0:T(8,128)(2,1)S(1)}, bf16[1024,768]{1,0:T(8,128)(2,1)}, u32[]{:S(2)}) copy-start(bf16[1024,768]{1,0:T(8,128)(2,1)} %get-tuple-element.44) | copy-start | bytes 4718596
  319.2 2.0 copy-start.1

commit v2 on v1

--- a/solution.py
+++ b/solution.py
@@ -221,6 +221,19 @@
             pltpu.make_async_copy(rows, rows, k.GS.at[hop, p]).wait()
             pltpu.make_async_copy(rows, rows, k.GR.at[hop, p]).wait()
 
+    G_LAG = (0, 2, 3)
+
+    def g_tick(t):
+        for hop in range(2, -1, -1):
+            q = t - G_LAG[hop]
+
+            def do(hop=hop, q=q):
+                g_wait(hop, q + NQP + 1)
+                if hop < 2:
+                    g_start(hop + 1, q + NQP + 1)
+
+            guarded(both(q >= 0, q < d.NJ), do)
+
     own_q = pltpu.make_async_copy(wq, k.WQ.at[pl.ds(s * d.DH, d.DH), :], k.LS.at[1])
     own_q.start()
     for p in range(NQP + 1):
@@ -306,7 +319,11 @@
             k.QKV[rows, part * d.D:(part + 1) * d.D] = y
         return 0
 
+    g_wait(0, NQP)
+    g_start(1, NQP)
     lax.fori_loop(0, d.M // RB, qkv_rows, 0)
+    g_wait(1, NQP)
+    g_start(2, NQP)
 
     lane = lax.broadcasted_iota(jnp.int32, (1, LANES), 1)
     head_mask = [lane < HEAD_DIM, lane >= HEAD_DIM]
@@ -321,26 +338,14 @@
         cols = [pl.ds(pl.multiple_of(part * d.D + hp * LANES, LANES), LANES) for part in range(3)]
         return rows, cols
 
-    g_wait(0, NQP)
-    g_start(1, NQP)
-    g_wait(1, NQP)
-    g_start(2, NQP)
-    g_wait(2, NQP)
-
     def attend_loop(u, _):
         attend_body(u)
-        return 0
-
-    def g_block_tick(p):
-        for hop in range(2, -1, -1):
-            q = p - hop
-
-            def do(hop=hop, q=q):
-                g_wait(hop, q)
-                if hop < 2:
-                    g_start(hop + 1, q)
-
-            guarded(jnp.logical_and(q > NQP, q < NG), do)
+
+        def do():
+            g_tick(lax.div(u, 2))
+
+        pl.when(lax.rem(u, 2) == 1)(do)
+        return 0
 
     def attend_body(u):
         seq, hp = lax.div(u, d.NH2), lax.rem(u, d.NH2)
@@ -362,10 +367,10 @@
                 total = part if total is None else total + part
             out_rows = pl.ds(pl.multiple_of(seq * SEQ_LEN + i * QB, QB), QB)
             k.ATT[out_rows, pl.ds(pl.multiple_of(hp * LANES, LANES), LANES)] = total.astype(BF16)
-        g_block_tick(u + NQP + 1)
 
     lax.fori_loop(0, d.NSEQ * d.NH2, attend_loop, 0)
     own_p.wait()
+    g_wait(2, NQP)
 
     HB = 128
 
@@ -379,8 +384,10 @@
         k.N2[rows, :] = n2
         k.N2T[:, rows] = n2.T
         k.DN2[rows, :] = jnp.zeros((HB, d.D), F32)
-        return 0
-
+        pl.when(lax.rem(i, 4) == 3)(lambda: g_tick(n_att + lax.div(i, 4)))
+        return 0
+
+    n_att = d.NSEQ * d.NH2 // 2
     lax.fori_loop(0, d.M // HB, hres_rows, 0)
     ccopy.wait()
 
@@ -485,8 +492,12 @@
     C1, C3 = GELU_C, GELU_C * 0.044715
     S1, S3 = 2.0 * GELU_C, 2.0 * GELU_C * 0.134145
 
+    g_done = n_att + d.M // HB // 4
+    assert g_done >= G_LAG[2]
+
     def mlp(j, _):
         wait_own(j)
+        g_tick(j + g_done)
         fcb = jnp.concatenate(
             [v[:, pl.ds(pl.multiple_of(f_at + j * LANES, LANES), LANES)] for v in (k.VA, k.VB)], axis=1
         )
@@ -521,10 +532,6 @@
         tick(2 * j + 1)
         return 0
 
-    g_wait(1, NG - 1)
-    g_start(2, NG - 1)
-    g_wait(2, NG - 2)
-    g_wait(2, NG - 1)
     lax.fori_loop(0, d.NJ, mlp, 0)
 
     g2 = full("ln2g")
@@ -714,7 +721,10 @@
 
 def per_device(d, tok, g1, be1, wq, qvb, wp, pb, g2, be2, wf, fb, wo, ob, cot):
     names, scratch = scratch_of(d)
-    vec = jnp.concatenate([v.astype(F32) for v in (g1, be1, qvb, pb, g2, be2, ob, fb)]).reshape(1, d.NV)
+    vec = sum(
+        lax.pad(v.astype(F32), jnp.zeros((), F32), [(at, d.NV - at - n, 0)])
+        for v, (at, n) in zip((g1, be1, qvb, pb, g2, be2, ob, fb), d.off.values())
+    ).reshape(1, d.NV)
     hbm = pl.BlockSpec(memory_space=pl.ANY)
     vmem = pl.BlockSpec(memory_space=pltpu.VMEM)
     out, dx, gr, vo = pl.pallas_call(
@@ -733,18 +743,104 @@
         ),
         name="block",
     )(tok, cot, wq, wp, wf, wo, vec)
-    vo = vo.reshape(d.NV)
-    v = {n: vo[at:at + size] for n, (at, size) in d.off.items()}
-    NJ, NP, PR, PO = d.NJ, d.NP, d.PR, d.PO
-    mlp = gr[:2 * NJ].reshape(NJ, 2, 8, 2, PR, LANES)
-    g_out = mlp[:, 0].reshape(NJ, 8, 2, PR // PO, PO, LANES).transpose(0, 1, 4, 2, 3, 5).reshape(d.FH, d.D)
-    g_fc = mlp[:, 1].transpose(1, 3, 2, 0, 4).reshape(d.DH, d.FF)
-    g_p = gr[2 * NJ:d.V0].transpose(1, 3, 0, 2, 4).reshape(d.DH, d.D)
-    g_q = gr[d.V0:].reshape(NP, 3, 8, 2, PR, LANES).transpose(2, 4, 1, 0, 3, 5).reshape(d.DH, 3 * d.D)
+    vecs_out = tuple(jax.ShapeDtypeStruct((n,), F32) for _, n in d.off.values())
+    g_q, g_p, g_fc, g_out, *v = pl.pallas_call(
+        functools.partial(finish_kernel, d),
+        out_shape=tuple(
+            jax.ShapeDtypeStruct(shape, F32)
+            for shape in ((d.DH, 3 * d.D), (d.DH, d.D), (d.DH, d.FF), (d.FH, d.D))
+        ) + vecs_out,
+        in_specs=[hbm, vmem],
+        out_specs=(hbm,) * 4 + (vmem,) * len(vecs_out),
+        scratch_shapes=[
+            pltpu.VMEM((d.NCH, 8, 2, d.PR, LANES), BF16),
+            pltpu.VMEM((2 * d.NJ + 8 * d.NP, d.DH, LANES), F32),
+            pltpu.VMEM((d.NJ, LANES, d.D), F32),
+            pltpu.SemaphoreType.DMA((d.NCH,)),
+            pltpu.SemaphoreType.DMA((d.NCH,)),
+        ],
+        compiler_params=pltpu.CompilerParams(vmem_limit_bytes=67_043_328),
+        name="finish",
+    )(gr, vo)
+    v = dict(zip(d.off, v))
     return (
-        out, dx, v["ln1g"], v["ln1b"], g_q.astype(F32), v["qvb"], g_p.astype(F32), v["projb"],
-        v["ln2g"], v["ln2b"], g_fc.astype(F32), v["fcb"], g_out.astype(F32), v["outb"],
+        out, dx, v["ln1g"], v["ln1b"], g_q, v["qvb"], g_p, v["projb"],
+        v["ln2g"], v["ln2b"], g_fc, v["fcb"], g_out, v["outb"],
     )
+
+
+def finish_kernel(d, gr, vo, g_q, g_p, g_fc, g_out, *refs):
+    outs, (G, C, O, si, so) = refs[:len(d.off)], refs[len(d.off):]
+    for ref, (at, n) in zip(outs, d.off.values()):
+        ref[...] = vo[0, at:at + n]
+
+    def load(c, _):
+        pltpu.make_async_copy(gr.at[c], G.at[c], si.at[c]).start()
+        return 0
+
+    lax.fori_loop(0, d.NCH, load, 0)
+
+    def arrived(c):
+        pltpu.make_async_copy(gr.at[c], G.at[c], si.at[c]).wait()
+
+    def cols_of(c, slot):
+        arrived(c)
+        for z in range(2):
+            for p in range(8):
+                C[slot + z, p * d.PR:(p + 1) * d.PR, :] = G[c, p, z].astype(F32)
+
+    per = d.D // LANES // 2
+
+    def out_copy(j):
+        return pltpu.make_async_copy(O.at[j], g_out.at[pl.ds(mult(j * LANES, LANES), LANES), :], so.at[2 * j])
+
+    def col_copies(dst, slot, cols, sem):
+        return [
+            pltpu.make_async_copy(C.at[slot + z], dst.at[:, pl.ds(mult(col, LANES), LANES)], sem)
+            for z, col in enumerate(cols)
+        ]
+
+    def fc_copies(j):
+        return col_copies(g_fc, 2 * j, (j * LANES, d.FH + j * LANES), so.at[2 * j + 1])
+
+    def wide_copies(i):
+        c, slot = 2 * d.NJ + i, 2 * (d.NJ + i)
+        if i < d.NP:
+            return col_copies(g_p, slot, (i * BLK, i * BLK + LANES), so.at[c])
+        grp, part = divmod(i - d.NP, 3)
+        col = part * d.D + grp * BLK
+        return col_copies(g_q, slot, (col, col + LANES), so.at[c])
+
+    def mlp(j, _):
+        c = 2 * j
+        arrived(c)
+        for p in range(8):
+            for t in range(2 * per):
+                O[j, p * d.PO:(p + 1) * d.PO, t * LANES:(t + 1) * LANES] = G[
+                    c, p, t // per, (t % per) * d.PO:(t % per + 1) * d.PO, :
+                ].astype(F32)
+        out_copy(j).start()
+        cols_of(c + 1, 2 * j)
+        for copy in fc_copies(j):
+            copy.start()
+        return 0
+
+    lax.fori_loop(0, d.NJ, mlp, 0)
+    for i in range(4 * d.NP):
+        cols_of(2 * d.NJ + i, 2 * (d.NJ + i))
+        for copy in wide_copies(i):
+            copy.start()
+
+    def drain(j, _):
+        out_copy(j).wait()
+        pair = C.at[pl.ds(0, 2)]
+        pltpu.make_async_copy(pair, pair, so.at[2 * j + 1]).wait()
+        return 0
+
+    lax.fori_loop(0, d.NJ, drain, 0)
+    for i in range(4 * d.NP):
+        pair = C.at[pl.ds(0, 2)]
+        pltpu.make_async_copy(pair, pair, so.at[2 * d.NJ + i]).wait()
 
 
 def solution(mesh):

time: 323 us -> 243 us (0.75)
  local copies, waits for them, and re-layouts: 51.4 us -> 4.54 us
  Pallas kernels: 262 us -> 236 us
  other arithmetic: 8.07 us -> 0.81 us
    pallas_call x1, Pallas kernels: 262 us -> 228 us  [per_device(): pl.pallas_call(functools.partial(block_kernel, d, names), out_shape=(jax....]
    convert_element_type x7 -> x0, local copies, waits for them, and re-layouts: 29.2 us -> none  [the longest x2 14 us: per_device(): g_out.astype(F32)]
    slice x6 -> x0, local copies, waits for them, and re-layouts: 11.8 us -> none  [the longest x3 3.92 us: per_device(): v = {n: vo[at:at + size] for n, (at, size) in d.off.items()}]
    pallas_call x0 -> x1, Pallas kernels: none -> 8.85 us  [per_device(): pl.pallas_call(functools.partial(finish_kernel, d), out_shape=tuple((jax....]
    convert_element_type x4 -> x0, other arithmetic: 8.07 us -> none  [the longest x1 4.13 us: per_device(): g_fc.astype(F32)]
    unnamed x15 -> x4, local copies, waits for them, and re-layouts: 9.14 us -> 3.92 us
where the time goes in v2:
time: 243 us; the launch traced here: 242 us
  Pallas kernels  236 us (97%)
  local copies, waits for them, and re-layouts  4.54 us (2%)
    pallas_call x1, Pallas kernels, per_device(): pl.pallas_call(functools.partial(block_kernel, d, names), out_shape=(jax....  228 us
    pallas_call x1, Pallas kernels, per_device(): pl.pallas_call(functools.partial(finish_kernel, d), out_shape=tuple((jax....  8.85 us

profile of v2, /device:TPU:0, one launch (start us, length us, event | category | flops | bytes accessed | tf_op | source)
XLA Modules:
  0.0 242.4 jit_solution(6401700418400800135)
XLA Ops:
  0.6 0.8 convert_add_fusion
  1.5 0.6 reshape.31.vec
  2.1 227.6 %block.1 = (bf16[1024,768]{1,0:T(8,128)(2,1)}, bf16[1024,768]{1,0:T(8,128)(2,1)}, bf16[36,8,2,48,128]{4,3,2,1,0:T(8,128)(2,1)}, f32[1,4608]{1,0:T(1,128)}) custom-call(bf16[1024,768]{1,0:T(8,128)(2,1)} %tok.1, bf16[1024,768]{1,0:T(8,128)(2,1)} %cot.1, bf16[384,2304]{1,0:T(8,128)(2,1)} %wq.1, bf16[384,768]{1,0:T(8,128)(2,1)} %wp.1, bf16[384,3072]{1,0:T(8,128)(2,1)} %wf.1, ...), custom_call_target="tpu_custom_call" | custom-call | tf_op jit(solution)/shard_map/block/pallas_call | solution.py:730
  229.6 8.9 %finish.1 = (f32[384,2304]{1,0:T(8,128)}, f32[384,768]{1,0:T(8,128)}, f32[384,3072]{1,0:T(8,128)}, f32[1536,768]{1,0:T(8,128)}, f32[384]{0:T(512)}, /*index=5*/f...) custom-call(bf16[36,8,2,48,128]{4,3,2,1,0:T(8,128)(2,1)} %get-tuple-, ...), custom_call_target="tpu_custom_call" | custom-call | tf_op jit(solution)/shard_map/finish/pallas_call | solution.py:747
  238.5 0.0 copy-start
  238.5 2.8 %copy.30 = bf16[1024,768]{1,0:T(8,128)(2,1)} copy(bf16[1024,768]{1,0:T(8,128)(2,1)} %get-tuple-element.60) | data formatting | bytes 3145728
  241.3 0.0 copy-done
  241.3 1.1 copy.31
Async XLA Ops:
  238.5 2.8 %copy-start = (bf16[1024,768]{1,0:T(8,128)(2,1)S(1)}, bf16[1024,768]{1,0:T(8,128)(2,1)}, u32[]{:S(2)}) copy-start(bf16[1024,768]{1,0:T(8,128)(2,1)} %get-tuple-element.61) | copy-start | bytes 4718596

commit v3 on v2

--- a/solution.py
+++ b/solution.py
@@ -41,7 +41,8 @@
         at += d.off[name][1]
     d.NV = at
     d.lag = [2, 3, 3, 2, 2] + [2] * (d.nb - 4) + [2, 2, 3, 2]
-    d.NS = 2 * max(d.lag)
+    d.NS = [2 * lag for lag in d.lag]
+    d.NSX = max(d.NS)
     d.first_ag = d.nb + 1
     d.B, d.E, at = [], [], 0
     for i, lag in enumerate(d.lag + [2]):
@@ -66,14 +67,14 @@
         ("WQ", vm((d.D, 3 * d.D), BF16)),
         ("WP", vm((d.D, d.D), BF16)),
         ("WF", vm((d.NJ, d.D, BLK), BF16)),
-        ("WO", vm((d.NJ, BLK, d.D), BF16)),
+        ("WO", vm((d.FF, d.D), BF16)),
         ("ACC", vm((d.NCH, 2, 8) + P8, BF16)),
-        ("R0", vm((d.NS, 2, 4) + P8, BF16)),
-        ("R1", vm((d.NS, 4) + P8, BF16)),
-        ("R2", vm((d.NS, 2) + P8, BF16)),
-        ("R3", vm((d.NS, 1) + P8, BF16)),
-        ("R4", vm((d.NS, d.PR, LANES), BF16)),
-        ("RX", vm((max(n_x, 1), d.NS, d.PR, LANES), BF16)),
+        ("R0", vm((d.NS[0], 2, 4) + P8, BF16)),
+        ("R1", vm((d.NS[1], 4) + P8, BF16)),
+        ("R2", vm((d.NS[2], 2) + P8, BF16)),
+        ("R3", vm((d.NS[3], 1) + P8, BF16)),
+        ("R4", vm((d.NS[4], d.PR, LANES), BF16)),
+        ("RX", vm((max(n_x, 1), d.NSX, d.PR, LANES), BF16)),
         ("QKV", vm((d.M, 3 * d.D), BF16)),
         ("T", vm((d.M, d.D), BF16)),
         ("COT", vm((d.M, d.D), BF16)),
@@ -84,6 +85,7 @@
         ("HRES", vm((d.M, d.D), F32)),
         ("OUTACC", vm((d.M, d.D), F32)),
         ("DN2", vm((d.M, d.D), F32)),
+        ("ACT", vm((d.M, d.FF), BF16)),
         ("ACTT", vm((BLK, d.M), BF16)),
         ("DPRE", vm((d.M, BLK), BF16)),
         ("VA", vm((1, d.NV), F32)),
@@ -94,9 +96,9 @@
         ("LS", sem((4 + d.NJ,))),
         ("GS", sem((3, d.NQP + 1 + d.NJ))),
         ("GR", sem((3, d.NQP + 1 + d.NJ))),
-        ("SS", sem((len(d.lag), d.NS))),
-        ("SR", sem((len(d.lag), d.NS))),
-        ("OS", sem((d.NS,))),
+        ("SS", sem((len(d.lag), d.NSX))),
+        ("SR", sem((len(d.lag), d.NSX))),
+        ("OS", sem((d.NSX,))),
         ("CR", pltpu.SemaphoreType.REGULAR((4,))),
         ("VS", sem((d.nb + 2,))),
         ("VQ", sem((d.nb + 2,))),
@@ -195,15 +197,15 @@
                 ))
             pairs.append((
                 wo.at[pl.ds(mult(j * LANES + g * OR, OR), OR), :],
-                k.WO.at[j, pl.ds(s * LANES + g * OR, OR), :],
+                k.WO.at[pl.ds(j * BLK + s * LANES + g * OR, OR), :],
             ))
             return pairs
         if hop == 1:
             fa = k.WF.at[j, pl.ds(o * d.DH + g * QR, QR), :]
-            oa = k.WO.at[j, pl.ds(o * LANES + g * OR, OR), :]
+            oa = k.WO.at[pl.ds(j * BLK + o * LANES + g * OR, OR), :]
         else:
             fa = k.WF.at[j, pl.ds(o * d.DH + b0 * 2 * QR, 2 * QR), :]
-            oa = k.WO.at[j, pl.ds(o * LANES + b0 * 2 * OR, 2 * OR), :]
+            oa = k.WO.at[pl.ds(j * BLK + o * LANES + b0 * 2 * OR, 2 * OR), :]
         return [(fa, fa), (oa, oa)]
 
     hop_peer = [x_peer, rep_peer(1), rep_peer(0)]
@@ -258,7 +260,7 @@
             ).start()
         pltpu.make_async_copy(
             wo.at[pl.ds(mult(j * LANES, LANES), LANES), :],
-            k.WO.at[j, pl.ds(s * LANES, LANES), :],
+            k.WO.at[pl.ds(j * BLK + s * LANES, LANES), :],
             k.LS.at[4 + j],
         ).start()
         return 0
@@ -294,34 +296,55 @@
 
     lax.fori_loop(0, d.M // LR, norm1, 0)
     own_q.wait()
-    for p in range(NQP + 2):
-        for hop in range(2, -1, -1):
-            if 0 <= p - hop < NQP:
-                g_wait(hop, p - hop)
-                if hop < 2:
-                    g_start(hop + 1, p - hop)
-
-    bq = k.VA[:, d.off["qvb"][0]:d.off["qvb"][0] + d.D]
-    bv = k.VB[:, d.off["qvb"][0]:d.off["qvb"][0] + d.D]
     RB = 256
-
-    def qkv_rows(i, _):
-        rows = pl.ds(pl.multiple_of(i * RB, RB), RB)
-        x = k.N1[rows, :]
-        for part in range(3):
-            y = nn(x, k.WQ[:, part * d.D:(part + 1) * d.D])
+    partial = (k.HRES, k.OUTACC, k.DN2)
+    own_cols = pl.ds(pl.multiple_of(s * d.DH, LANES), d.DH)
+    oth_cols = pl.ds(pl.multiple_of(o * d.DH, LANES), d.DH)
+    own_rows, oth_rows = pl.ds(s * d.DH, d.DH), pl.ds(o * d.DH, d.DH)
+
+    def own_part(part):
+        def step(i, _):
+            rows = pl.ds(pl.multiple_of(i * RB, RB), RB)
+            partial[part][rows, :] = nn(k.N1[rows, own_cols], k.WQ[own_rows, part * d.D:(part + 1) * d.D])
+            return 0
+
+        lax.fori_loop(0, d.M // RB, step, 0)
+
+    per_part = NQP // 3
+
+    def oth_piece(p):
+        part, col = p // per_part, p % per_part * d.QW
+        bias = None
+        if part != 1:
+            at = d.off["qvb"][0] + col
+            bias = (k.VA if part == 0 else k.VB)[:, at:at + d.QW]
+
+        def step(i, _):
+            rows = pl.ds(pl.multiple_of(i * RB, RB), RB)
+            y = nn(k.N1[rows, oth_cols], k.WQ[oth_rows, p * d.QW:(p + 1) * d.QW]) + partial[part][rows, col:col + d.QW]
+            y = (y if bias is None else y + bias).astype(BF16)
             if part == 0:
-                y = (y + bq).astype(BF16) * jnp.asarray(HEAD_DIM ** -0.5, BF16)
-            elif part == 1:
-                y = y.astype(BF16)
-            else:
-                y = (y + bv).astype(BF16)
-            k.QKV[rows, part * d.D:(part + 1) * d.D] = y
-        return 0
-
+                y = y * jnp.asarray(HEAD_DIM ** -0.5, BF16)
+            k.QKV[rows, p * d.QW:(p + 1) * d.QW] = y
+            return 0
+
+        lax.fori_loop(0, d.M // RB, step, 0)
+
+    for p in range(NQP):
+        g_wait(0, p)
+        g_start(1, p)
+        if p % per_part == 0:
+            own_part(p // per_part)
+    for p in range(NQP):
+        g_wait(1, p)
+        g_start(2, p)
+        if p:
+            g_wait(2, p - 1)
+            oth_piece(p - 1)
     g_wait(0, NQP)
     g_start(1, NQP)
-    lax.fori_loop(0, d.M // RB, qkv_rows, 0)
+    g_wait(2, NQP - 1)
+    oth_piece(NQP - 1)
     g_wait(1, NQP)
     g_start(2, NQP)
 
@@ -339,12 +362,9 @@
         return rows, cols
 
     def attend_loop(u, _):
-        attend_body(u)
-
-        def do():
-            g_tick(lax.div(u, 2))
-
-        pl.when(lax.rem(u, 2) == 1)(do)
+        attend_body(2 * u)
+        attend_body(2 * u + 1)
+        g_tick(u)
         return 0
 
     def attend_body(u):
@@ -368,27 +388,26 @@
             out_rows = pl.ds(pl.multiple_of(seq * SEQ_LEN + i * QB, QB), QB)
             k.ATT[out_rows, pl.ds(pl.multiple_of(hp * LANES, LANES), LANES)] = total.astype(BF16)
 
-    lax.fori_loop(0, d.NSEQ * d.NH2, attend_loop, 0)
+    lax.fori_loop(0, d.NSEQ * d.NH2 // 2, attend_loop, 0)
     own_p.wait()
     g_wait(2, NQP)
 
-    HB = 128
+    HA = SEQ_LEN
 
     def hres_rows(i, _):
-        rows = pl.ds(pl.multiple_of(i * HB, HB), HB)
+        rows = pl.ds(pl.multiple_of(i * HA, HA), HA)
         h = k.T[rows, :].astype(F32) + nn(k.ATT[rows, :], k.WP[...]) + full("projb")
         k.HRES[rows, :] = h
-        k.OUTACC[rows, :] = h + full("outb")
         xhat, _r = norm_rows(h)
         n2 = (xhat * full("ln2g") + full("ln2b")).astype(BF16)
         k.N2[rows, :] = n2
         k.N2T[:, rows] = n2.T
-        k.DN2[rows, :] = jnp.zeros((HB, d.D), F32)
-        pl.when(lax.rem(i, 4) == 3)(lambda: g_tick(n_att + lax.div(i, 4)))
+        k.DN2[rows, :] = jnp.zeros((HA, d.D), F32)
+        g_tick(n_att + i)
         return 0
 
     n_att = d.NSEQ * d.NH2 // 2
-    lax.fori_loop(0, d.M // HB, hres_rows, 0)
+    lax.fori_loop(0, d.M // HA, hres_rows, 0)
     ccopy.wait()
 
     def cot_sum(i, total):
@@ -403,7 +422,7 @@
     last = len(d.lag)
 
     def stage(i, c):
-        slot = lax.rem(c, d.NS)
+        slot = lax.rem(c, d.NS[i])
         sems = (k.SS.at[i, slot], k.SR.at[i, slot])
         A = k.ACC
         if i == 0:
@@ -439,7 +458,7 @@
         return c, ok
 
     def out_copy(c):
-        return pltpu.make_async_copy(k.ACC.at[c, s], gr_o.at[c], k.OS.at[lax.rem(c, d.NS)])
+        return pltpu.make_async_copy(k.ACC.at[c, s], gr_o.at[c], k.OS.at[lax.rem(c, d.NSX)])
 
     def begin(i, c):
         if i == last:
@@ -489,10 +508,11 @@
                     ]
 
     f_at = d.off["fcb"][0]
+    MB = SEQ_LEN
     C1, C3 = GELU_C, GELU_C * 0.044715
     S1, S3 = 2.0 * GELU_C, 2.0 * GELU_C * 0.134145
 
-    g_done = n_att + d.M // HB // 4
+    g_done = n_att + d.M // HA
     assert g_done >= G_LAG[2]
 
     def mlp(j, _):
@@ -502,9 +522,9 @@
             [v[:, pl.ds(pl.multiple_of(f_at + j * LANES, LANES), LANES)] for v in (k.VA, k.VB)], axis=1
         )
 
-        def rows_step(i, total):
-            rows = pl.ds(pl.multiple_of(i * RB, RB), RB)
-            wfj, woj = k.WF[j], k.WO[j]
+        def rows_step(i):
+            rows = pl.ds(i * MB, MB)
+            wfj, woj = k.WF[j], k.WO[pl.ds(pl.multiple_of(j * BLK, BLK), BLK), :]
             c = k.COT[rows, :]
             pre = nn(k.N2[rows, :], wfj) + fcb
             d_act = nt(c, woj)
@@ -516,11 +536,11 @@
             ab, db = a.astype(BF16), d_pre.astype(BF16)
             k.ACTT[:, rows] = ab.T
             k.DPRE[rows, :] = db
-            k.OUTACC[rows, :] += nn(ab, woj)
+            k.ACT[rows, pl.ds(pl.multiple_of(j * BLK, BLK), BLK)] = ab
             k.DN2[rows, :] += nt(db, wfj)
-            return total + jnp.sum(d_pre, axis=0, keepdims=True)
-
-        total = lax.fori_loop(0, d.M // RB, rows_step, jnp.zeros((1, BLK), F32))
+            return jnp.sum(d_pre, axis=0, keepdims=True)
+
+        total = sum(rows_step(i) for i in range(d.M // MB))
         at = pl.ds(pl.multiple_of(f_at + j * LANES, LANES), LANES)
         k.VG[0, :, at] = total[:, :LANES]
         k.VG[1, :, at] = total[:, LANES:]
@@ -538,7 +558,6 @@
 
     def norm2_back(i, sums):
         rows = pl.ds(pl.multiple_of(i * LR, LR), LR)
-        k.N1[rows, :] = k.OUTACC[rows, :].astype(BF16)
         xhat, r = norm_rows(k.HRES[rows, :])
         dn = k.DN2[rows, :]
         gg = dn * g2
@@ -555,15 +574,13 @@
     put_vec("ln2g", sums[0])
     put_vec("ln2b", sums[1])
     put_vec("projb", sums[2])
-    bcopy = pltpu.make_async_copy(k.N1, out_o, k.LS.at[0])
-    bcopy.start()
 
     def transpose_att(i, _):
-        rows = pl.ds(pl.multiple_of(i * HB, HB), HB)
+        rows = pl.ds(pl.multiple_of(i * HA, HA), HA)
         k.N2T[:, rows] = k.ATT[rows, :].T
         return 0
 
-    lax.fori_loop(0, d.M // HB, transpose_att, 0)
+    lax.fori_loop(0, d.M // HA, transpose_att, 0)
 
     def proj_cols(n, _):
         c = 2 * d.NJ + n
@@ -574,7 +591,6 @@
         return 0
 
     lax.fori_loop(0, d.NP, proj_cols, 0)
-    bcopy.wait()
 
     def att_rows(i, _):
         rows = pl.ds(pl.multiple_of(i * RB, RB), RB)
@@ -586,12 +602,12 @@
     g1, be1 = full("ln1g"), full("ln1b")
 
     def transpose_n1(i, _):
-        rows = pl.ds(pl.multiple_of(i * HB, HB), HB)
+        rows = pl.ds(pl.multiple_of(i * HA, HA), HA)
         xhat, _r = norm_rows(k.T[rows, :].astype(F32))
         k.N2T[:, rows] = (xhat * g1 + be1).astype(BF16).T
         return 0
 
-    lax.fori_loop(0, d.M // HB, transpose_n1, 0)
+    lax.fori_loop(0, d.M // HA, transpose_n1, 0)
 
     def attend_back(seq, hp):
         rows, cols = unit_refs(seq, hp)
@@ -642,13 +658,6 @@
         at, n = d.off["qvb"]
         k.VG[half, :, at:at + n] = jnp.zeros((1, n), F32)
 
-    def zero_dn1(i, _):
-        rows = pl.ds(pl.multiple_of(i * LR, LR), LR)
-        k.OUTACC[rows, :] = jnp.zeros((LR, d.D), F32)
-        return 0
-
-    lax.fori_loop(0, d.M // LR, zero_dn1, 0)
-
     def group(grp, _):
         v0 = d.V0 + grp * d.GV
 
@@ -665,12 +674,6 @@
             for sh in range(2):
                 put_cols(c, sh, nn(k.N2T[sh * d.DH:(sh + 1) * d.DH, :], k.QKV[:, cols]))
 
-            def rows_step(i, _):
-                rows = pl.ds(pl.multiple_of(i * RB, RB), RB)
-                k.OUTACC[rows, :] += nt(k.QKV[rows, cols], k.WQ[:, cols])
-                return 0
-
-            lax.fori_loop(0, d.M // RB, rows_step, 0)
             tick(v0 + d.GU + part)
             return 0
 
@@ -679,19 +682,24 @@
 
     lax.fori_loop(0, d.NP, group, 0)
 
+    HB, TB = 256, 2
+    NB = d.M // HB
+
     def norm1_back(i, sums):
-        rows = pl.ds(pl.multiple_of(i * LR, LR), LR)
+        rows = pl.ds(pl.multiple_of(i * HB, HB), HB)
+        dn = nt(k.QKV[rows, :], k.WQ[...])
         xhat, r = norm_rows(k.T[rows, :].astype(F32))
-        dn = k.OUTACC[rows, :]
         gg = dn * g1
         dx = k.DN2[rows, :] + r * (
             gg - jnp.mean(gg, axis=-1, keepdims=True) - xhat * jnp.mean(gg * xhat, axis=-1, keepdims=True)
         )
         k.COT[rows, :] = dx.astype(BF16)
         add = lambda v: jnp.sum(v, axis=0, keepdims=True)
+        for u in range(TB):
+            tick(d.NVS + TB * i + u)
         return sums[0] + add(dn * xhat), sums[1] + add(dn)
 
-    sums = lax.fori_loop(0, d.M // LR, norm1_back, (zrow, zrow))
+    sums = lax.fori_loop(0, NB, norm1_back, (zrow, zrow))
     put_vec("ln1g", sums[0])
     put_vec("ln1b", sums[1])
     xcopy = pltpu.make_async_copy(k.COT, dx_o, k.LS.at[0])
@@ -702,21 +710,43 @@
         peer = x_peer if i == 0 else rep_peer(i - 1)
         return remote(src, k.VR.at[i], k.VS.at[i], k.VQ.at[i], peer)
 
-    end = d.NVS + d.E[-1]
     n_v = d.nb + 1
+
+    def vec_step(i):
+        vec_copy(i).wait()
+        k.VG[s] = k.VG[s] + k.VR[i]
+        if i + 1 < n_v:
+            vec_copy(i + 1).start()
+
     vec_copy(0).start()
-    step = 0
-    for t in range(d.NVS, end):
+    bout = full("outb")
+
+    def out_step(i, _):
+        @pl.when(i < NB)
+        def _():
+            rows = pl.ds(pl.multiple_of(i * HB, HB), HB)
+            y = k.HRES[rows, :] + nn(k.ACT[rows, :], k.WO[...]) + bout
+            k.N2[rows, :] = y.astype(BF16)
+
+        for u in range(TB):
+            tick(d.NVS + TB * (NB + i) + u)
+        for v in range(n_v):
+            pl.when(i == v)(functools.partial(vec_step, v))
+        return 0
+
+    n_out = max(NB, n_v)
+    lax.fori_loop(0, n_out, out_step, 0)
+    bcopy = pltpu.make_async_copy(k.N2, out_o, k.LS.at[1])
+    bcopy.start()
+
+    def rest(t, _):
         tick(t)
-        if step < n_v and (t - d.NVS) % 2 == 1:
-            vec_copy(step).wait()
-            k.VG[s] = k.VG[s] + k.VR[step]
-            step += 1
-            if step < n_v:
-                vec_copy(step).start()
-    assert step == n_v
+        return 0
+
+    lax.fori_loop(d.NVS + TB * (NB + n_out), d.NVS + d.E[-1], rest, 0)
     vo_o[...] = k.VG[s]
     xcopy.wait()
+    bcopy.wait()
 
 
 def per_device(d, tok, g1, be1, wq, qvb, wp, pb, g2, be2, wf, fb, wo, ob, cot):

time: 243 us -> 207 us (0.85)
  Pallas kernels: 236 us -> 201 us
    pallas_call x1, Pallas kernels: 228 us -> 192 us  [per_device(): pl.pallas_call(functools.partial(block_kernel, d, names), out_shape=(jax....]
where the time goes in v3:
time: 207 us
  Pallas kernels  201 us (97%)
  local copies, waits for them, and re-layouts  4.54 us (2%)
    pallas_call x1, Pallas kernels, per_device(): pl.pallas_call(functools.partial(block_kernel, d, names), out_shape=(jax....  192 us
    pallas_call x1, Pallas kernels, per_device(): pl.pallas_call(functools.partial(finish_kernel, d), out_shape=tuple((jax....  8.85 us

profile of v3, /device:TPU:0, one launch (start us, length us, event | category | flops | bytes accessed | tf_op | source)
XLA Modules:
  0.0 206.6 jit_solution(10622702875508178764)
XLA Ops:
  0.6 0.8 convert_add_fusion
  1.5 0.6 reshape.31.vec
  2.1 191.8 %block.1 = (bf16[1024,768]{1,0:T(8,128)(2,1)}, bf16[1024,768]{1,0:T(8,128)(2,1)}, bf16[36,8,2,48,128]{4,3,2,1,0:T(8,128)(2,1)}, f32[1,4608]{1,0:T(1,128)}) custom-call(bf16[1024,768]{1,0:T(8,128)(2,1)} %tok.1, bf16[1024,768]{1,0:T(8,128)(2,1)} %cot.1, bf16[384,2304]{1,0:T(8,128)(2,1)} %wq.1, bf16[384,768]{1,0:T(8,128)(2,1)} %wp.1, bf16[384,3072]{1,0:T(8,128)(2,1)} %wf.1, ...), custom_call_target="tpu_custom_call" | custom-call | tf_op jit(solution)/shard_map/block/pallas_call | solution.py:760
  193.8 8.9 %finish.1 = (f32[384,2304]{1,0:T(8,128)}, f32[384,768]{1,0:T(8,128)}, f32[384,3072]{1,0:T(8,128)}, f32[1536,768]{1,0:T(8,128)}, f32[384]{0:T(512)}, /*index=5*/f...) custom-call(bf16[36,8,2,48,128]{4,3,2,1,0:T(8,128)(2,1)} %get-tuple-, ...), custom_call_target="tpu_custom_call" | custom-call | tf_op jit(solution)/shard_map/finish/pallas_call | solution.py:777
  202.7 0.0 copy-start
  202.7 2.8 %copy.30 = bf16[1024,768]{1,0:T(8,128)(2,1)} copy(bf16[1024,768]{1,0:T(8,128)(2,1)} %get-tuple-element.60) | data formatting | bytes 3145728
  205.5 0.0 copy-done
  205.5 1.1 copy.31
Async XLA Ops:
  202.7 2.8 %copy-start = (bf16[1024,768]{1,0:T(8,128)(2,1)S(1)}, bf16[1024,768]{1,0:T(8,128)(2,1)}, u32[]{:S(2)}) copy-start(bf16[1024,768]{1,0:T(8,128)(2,1)} %get-tuple-element.61) | copy-start | bytes 4718596

commit v4 on v3

--- a/solution.py
+++ b/solution.py
@@ -17,6 +17,7 @@
 LANES = 128
 BLK = 256
 NEG = -1e30
+DRAIN = (0, 0, 2, 1, 1, 1, 1, 1, 1)
 VECS = ("ln1g", "ln1b", "qvb", "projb", "ln2g", "ln2b", "outb", "fcb")
 
 
@@ -40,20 +41,21 @@
         d.off[name] = (at, half.get(name, width // 2))
         at += d.off[name][1]
     d.NV = at
-    d.lag = [2, 3, 3, 2, 2] + [2] * (d.nb - 4) + [2, 2, 3, 2]
+    d.lag = [1, 3, 2, 2] + [1] * (d.nb - 4) + [2, 2, 1]
     d.NS = [2 * lag for lag in d.lag]
     d.NSX = max(d.NS)
-    d.first_ag = d.nb + 1
+    d.first_ag = d.nb
     d.B, d.E, at = [], [], 0
-    for i, lag in enumerate(d.lag + [2]):
+    for i, lag in enumerate(d.lag + [1]):
         at += i == d.first_ag
         d.B.append(at)
         at += lag
         d.E.append(at)
-    d.V0 = 2 * d.NJ + d.NP
+    d.V0 = d.NJ + d.NP
     d.GU = 2 * d.NSEQ
-    d.GV = d.GU + 3
-    d.NVS = d.V0 + d.NP * d.GV
+    assert d.GU >= 3
+    d.VD = d.V0 + d.NP * d.GU
+    d.NVS = d.VD + 3
     d.NQP = 6
     d.QW = 3 * width // d.NQP
     return d
@@ -69,12 +71,11 @@
         ("WF", vm((d.NJ, d.D, BLK), BF16)),
         ("WO", vm((d.FF, d.D), BF16)),
         ("ACC", vm((d.NCH, 2, 8) + P8, BF16)),
-        ("R0", vm((d.NS[0], 2, 4) + P8, BF16)),
-        ("R1", vm((d.NS[1], 4) + P8, BF16)),
-        ("R2", vm((d.NS[2], 2) + P8, BF16)),
-        ("R3", vm((d.NS[3], 1) + P8, BF16)),
-        ("R4", vm((d.NS[4], d.PR, LANES), BF16)),
-        ("RX", vm((max(n_x, 1), d.NSX, d.PR, LANES), BF16)),
+        ("R0", vm((d.NS[0], 2, 2, 4) + P8, BF16)),
+        ("R1", vm((d.NS[1], 2, 4) + P8, BF16)),
+        ("R2", vm((d.NS[2], 2, 2) + P8, BF16)),
+        ("R3", vm((d.NS[3], 3, 2, d.PR, LANES), BF16)),
+        ("RX", vm((max(n_x, 1), d.NSX, 2, d.PR, LANES), BF16)),
         ("QKV", vm((d.M, 3 * d.D), BF16)),
         ("T", vm((d.M, d.D), BF16)),
         ("COT", vm((d.M, d.D), BF16)),
@@ -83,7 +84,6 @@
         ("N2", vm((d.M, d.D), BF16)),
         ("N2T", vm((d.D, d.M), BF16)),
         ("HRES", vm((d.M, d.D), F32)),
-        ("OUTACC", vm((d.M, d.D), F32)),
         ("DN2", vm((d.M, d.D), F32)),
         ("ACT", vm((d.M, d.FF), BF16)),
         ("ACTT", vm((BLK, d.M), BF16)),
@@ -96,10 +96,10 @@
         ("LS", sem((4 + d.NJ,))),
         ("GS", sem((3, d.NQP + 1 + d.NJ))),
         ("GR", sem((3, d.NQP + 1 + d.NJ))),
-        ("SS", sem((len(d.lag), d.NSX))),
-        ("SR", sem((len(d.lag), d.NSX))),
+        ("SS", sem((len(d.lag), d.NSX, 3))),
+        ("SR", sem((len(d.lag), d.NSX, 3))),
         ("OS", sem((d.NSX,))),
-        ("CR", pltpu.SemaphoreType.REGULAR((4,))),
+        ("CR", pltpu.SemaphoreType.REGULAR((5,))),
         ("VS", sem((d.nb + 2,))),
         ("VQ", sem((d.nb + 2,))),
     ]
@@ -158,6 +158,7 @@
 
     barrier = pltpu.get_barrier_semaphore()
     peers = [x_peer] + [rep_peer(i) for i in range(d.nb)]
+    peers.append({"rep": rep + (1 - 2 * b2) * 4 + (1 - 2 * b3) * 8, "shard": s})
     for peer in peers:
         pl.semaphore_signal(barrier, inc=1, device_id=peer, device_id_type=MESH)
     pl.semaphore_wait(barrier, len(peers))
@@ -240,16 +241,12 @@
     own_q.start()
     for p in range(NQP + 1):
         g_start(0, p)
+    own_p = pltpu.make_async_copy(wp, k.WP.at[pl.ds(s * d.DH, d.DH), :], k.LS.at[2])
+    ccopy = pltpu.make_async_copy(cot, k.COT, k.LS.at[3])
 
     def start_blocks(j, _):
         g_start(0, j + NQP + 1)
         return 0
-
-    lax.fori_loop(0, d.NJ, start_blocks, 0)
-    own_p = pltpu.make_async_copy(wp, k.WP.at[pl.ds(s * d.DH, d.DH), :], k.LS.at[2])
-    own_p.start()
-    ccopy = pltpu.make_async_copy(cot, k.COT, k.LS.at[3])
-    ccopy.start()
 
     def start_own(j, _):
         for strip in range(2):
@@ -265,8 +262,6 @@
         ).start()
         return 0
 
-    lax.fori_loop(0, d.NJ, start_own, 0)
-
     def wait_own(j):
         pltpu.make_async_copy(k.WF.at[0], k.WF.at[0], k.LS.at[4 + j]).wait()
 
@@ -294,25 +289,16 @@
         k.N1[rows, :] = (xhat * full("ln1g") + full("ln1b")).astype(BF16)
         return 0
 
-    lax.fori_loop(0, d.M // LR, norm1, 0)
+    half = d.M // LR // 2
+    lax.fori_loop(0, half, norm1, 0)
+    g_wait(0, 0)
+    g_start(1, 0)
+    lax.fori_loop(half, 2 * half, norm1, 0)
     own_q.wait()
-    RB = 256
-    partial = (k.HRES, k.OUTACC, k.DN2)
-    own_cols = pl.ds(pl.multiple_of(s * d.DH, LANES), d.DH)
-    oth_cols = pl.ds(pl.multiple_of(o * d.DH, LANES), d.DH)
-    own_rows, oth_rows = pl.ds(s * d.DH, d.DH), pl.ds(o * d.DH, d.DH)
-
-    def own_part(part):
-        def step(i, _):
-            rows = pl.ds(pl.multiple_of(i * RB, RB), RB)
-            partial[part][rows, :] = nn(k.N1[rows, own_cols], k.WQ[own_rows, part * d.D:(part + 1) * d.D])
-            return 0
-
-        lax.fori_loop(0, d.M // RB, step, 0)
-
+    RB = 512
     per_part = NQP // 3
 
-    def oth_piece(p):
+    def qkv_piece(p):
         part, col = p // per_part, p % per_part * d.QW
         bias = None
         if part != 1:
@@ -321,7 +307,7 @@
 
         def step(i, _):
             rows = pl.ds(pl.multiple_of(i * RB, RB), RB)
-            y = nn(k.N1[rows, oth_cols], k.WQ[oth_rows, p * d.QW:(p + 1) * d.QW]) + partial[part][rows, col:col + d.QW]
+            y = nn(k.N1[rows, :], k.WQ[:, p * d.QW:(p + 1) * d.QW])
             y = (y if bias is None else y + bias).astype(BF16)
             if part == 0:
                 y = y * jnp.asarray(HEAD_DIM ** -0.5, BF16)
@@ -330,27 +316,37 @@
 
         lax.fori_loop(0, d.M // RB, step, 0)
 
-    for p in range(NQP):
+    own_p.start()
+    ccopy.start()
+    for p in range(1, NQP):
         g_wait(0, p)
         g_start(1, p)
-        if p % per_part == 0:
-            own_part(p // per_part)
-    for p in range(NQP):
-        g_wait(1, p)
-        g_start(2, p)
-        if p:
-            g_wait(2, p - 1)
-            oth_piece(p - 1)
-    g_wait(0, NQP)
-    g_start(1, NQP)
-    g_wait(2, NQP - 1)
-    oth_piece(NQP - 1)
+        if p >= 2:
+            g_wait(1, p - 2)
+            g_start(2, p - 2)
+        if p >= 4:
+            g_wait(2, p - 4)
+            qkv_piece(p - 4)
+        if p == 1:
+            lax.fori_loop(0, d.NJ, start_blocks, 0)
+        if p == NQP - 1:
+            lax.fori_loop(0, d.NJ, start_own, 0)
+    g_wait(1, NQP - 2)
+    g_start(2, NQP - 2)
+    for p in range(NQP - 4, NQP):
+        g_wait(2, p)
+        qkv_piece(p)
+        if p == 2:
+            g_wait(1, NQP - 1)
+            g_start(2, NQP - 1)
+            g_wait(0, NQP)
+            g_start(1, NQP)
     g_wait(1, NQP)
     g_start(2, NQP)
 
     lane = lax.broadcasted_iota(jnp.int32, (1, LANES), 1)
     head_mask = [lane < HEAD_DIM, lane >= HEAD_DIM]
-    zero = jnp.zeros((), BF16)
+    zero, one = jnp.zeros((), BF16), jnp.ones((), BF16)
     QB = 256
     NQB = SEQ_LEN // QB
     tri = lax.broadcasted_iota(jnp.int32, (QB, QB), 1) <= lax.broadcasted_iota(jnp.int32, (QB, QB), 0)
@@ -373,18 +369,18 @@
         q2, k2, v2 = (k.QKV[rows, c] for c in cols)
         for i in range(NQB):
             klen = (i + 1) * QB
-            total = None
+            parts = []
             for mask in head_mask:
                 qm = jnp.where(mask, q2[i * QB:klen], zero)
-                vm = jnp.where(mask, v2[:klen], zero)
+                vm = jnp.where(mask, v2[:klen], one)
                 sc = nt(qm, k2[:klen])
                 diag = jnp.where(tri, sc[:, klen - QB:], NEG)
                 sc = diag if i == 0 else jnp.concatenate([sc[:, :klen - QB], diag], axis=1)
                 top = jnp.max(sc, axis=1, keepdims=True)
                 e = jnp.exp(sc - top)
-                den = jnp.sum(e, axis=1, keepdims=True)
-                part = nn(e.astype(BF16), vm) * (1.0 / den)
-                total = part if total is None else total + part
+                parts.append(nn(e.astype(BF16), vm))
+            den = jnp.where(head_mask[0], *(pltpu.roll(p, HEAD_DIM, 1) for p in parts))
+            total = jnp.where(head_mask[0], *parts) / den
             out_rows = pl.ds(pl.multiple_of(seq * SEQ_LEN + i * QB, QB), QB)
             k.ATT[out_rows, pl.ds(pl.multiple_of(hp * LANES, LANES), LANES)] = total.astype(BF16)
 
@@ -421,74 +417,99 @@
     n_x = d.nb - 4
     last = len(d.lag)
 
-    def stage(i, c):
-        slot = lax.rem(c, d.NS[i])
-        sems = (k.SS.at[i, slot], k.SR.at[i, slot])
-        A = k.ACC
+    def quad_peer(q):
+        c2 = 1 - b2 if q & 1 else b2
+        c3 = 1 - b3 if q & 2 else b3
+        return {"rep": rep + (c2 - b2) * 4 + (c3 - b3) * 8, "shard": s}, c2, c3
+
+    def order(v, c, n):
+        return v if n == 2 else c - d.NJ
+
+    def stage(i, v, c, n):
+        slot = lax.rem(order(v, c, n), d.NS[i])
+        A, it, first = k.ACC, pl.ds(c, n), pl.ds(0, n)
         if i == 0:
-            return A.at[c, :, pl.ds(4 - lo4, 4)], k.R0.at[slot], sems, rep_peer(0), (A.at[c, :, pl.ds(lo4, 4)], k.R0.at[slot])
+            dst = k.R0.at[slot, first]
+            return [(A.at[it, :, pl.ds(4 - lo4, 4)], dst, rep_peer(0), 0)], A.at[it, :, pl.ds(lo4, 4)], [dst]
         if i == 1:
-            return A.at[c, o, pl.ds(lo4, 4)], k.R1.at[slot], sems, x_peer, (A.at[c, s, pl.ds(lo4, 4)], k.R1.at[slot])
+            dst = k.R1.at[slot, first]
+            return [(A.at[it, o, pl.ds(lo4, 4)], dst, x_peer, None)], A.at[it, s, pl.ds(lo4, 4)], [dst]
         if i == 2:
-            return (A.at[c, s, pl.ds(lo4 + 2 - 2 * b1, 2)], k.R2.at[slot], sems, rep_peer(1),
-                    (A.at[c, s, pl.ds(lo2, 2)], k.R2.at[slot]))
+            dst = k.R2.at[slot, first]
+            src = A.at[it, s, pl.ds(lo2 + 2 - 4 * b1, 2)]
+            return [(src, dst, rep_peer(1), 1)], A.at[it, s, pl.ds(lo2, 2)], [dst]
+        mine = A.at[it, s, lo1, b3]
         if i == 3:
-            return (A.at[c, s, pl.ds(lo2 + 1 - b2, 1)], k.R3.at[slot], sems, rep_peer(2),
-                    (A.at[c, s, pl.ds(lo1, 1)], k.R3.at[slot]))
-        if i == 4:
-            return A.at[c, s, lo1, 1 - b3], k.R4.at[slot], sems, rep_peer(3), (A.at[c, s, lo1, b3], k.R4.at[slot])
-        if i < 5 + n_x:
-            dst = k.RX.at[i - 5, slot]
-            return A.at[c, s, lo1, b3], dst, sems, rep_peer(i - 1), (A.at[c, s, lo1, b3], dst)
-        at = [A.at[c, s, lo1, b3], A.at[c, s, pl.ds(lo1, 1)], A.at[c, s, pl.ds(lo2, 2)], A.at[c, s, pl.ds(lo4, 4)]][i - 5 - n_x]
-        return at, at, sems, rep_peer(3 - (i - 5 - n_x)), None
-
-    def chunk_of(v):
-        w = v - d.V0
+            copies = []
+            for q in (1, 2, 3):
+                peer, c2, c3 = quad_peer(q)
+                copies.append((A.at[it, s, lo2 + c2, c3], k.R3.at[slot, q - 1, first], peer, 1 + q))
+            return copies, mine, [k.R3.at[slot, q, first] for q in range(3)]
+        if i < d.first_ag:
+            dst = k.RX.at[i - 4, slot, first]
+            return [(mine, dst, rep_peer(i), None)], mine, [dst]
+        if i == d.first_ag:
+            return [(mine, mine, quad_peer(q)[0], 1 + q) for q in (1, 2, 3)], None, None
+        bitno = 1 - (i - d.first_ag - 1)
+        at = A.at[it, s, pl.ds(lo2, 2)] if bitno == 1 else A.at[it, s, pl.ds(lo4, 4)]
+        return [(at, at, rep_peer(bitno), bitno)], None, None
+
+    def chunks_of(v, kinds):
         if isinstance(v, int):
-            if v < d.V0:
-                return v, 0 <= v
-            grp, r = divmod(w, d.GV)
-            return d.V0 + 3 * grp + r - d.GU, v < d.NVS and r >= d.GU
-        late = v >= d.V0
-        w = jnp.maximum(w, 0)
-        grp, r = lax.div(w, d.GV), lax.rem(w, d.GV)
-        c = jnp.where(late, d.V0 + 3 * grp + r - d.GU, v)
-        ok = jnp.logical_and(v >= 0, jnp.logical_and(v < d.NVS, jnp.logical_or(v < d.V0, r >= d.GU)))
-        return c, ok
-
-    def out_copy(c):
-        return pltpu.make_async_copy(k.ACC.at[c, s], gr_o.at[c], k.OS.at[lax.rem(c, d.NSX)])
-
-    def begin(i, c):
+            grp, r = divmod(max(v - d.V0, 0), d.GU)
+            found = [(0 <= v < d.NJ, 2 * v, 2), (d.NJ <= v < d.V0, v + d.NJ, 1)]
+            found.append((v >= d.V0 and v < d.NVS and grp > 0 and r < 3, 2 * d.NJ + d.NP + 3 * (grp - 1) + r, 1))
+            return [f for f in found if f[0]]
+        found = []
+        if 2 in kinds:
+            found.append((jnp.logical_and(v >= 0, v < d.NJ), 2 * v, 2))
+        if 1 in kinds:
+            w = jnp.maximum(v - d.V0, 0)
+            grp, r = lax.div(w, d.GU), lax.rem(w, d.GU)
+            late = v >= d.V0
+            c = jnp.where(late, 2 * d.NJ + d.NP + 3 * (grp - 1) + r, v + d.NJ)
+            ok = jnp.where(late, jnp.logical_and(grp > 0, r < 3), v >= d.NJ)
+            found.append((jnp.logical_and(ok, v < d.NVS), c, 1))
+        return found
+
+    def out_copy(v, c, n):
+        it = pl.ds(c, n)
+        return pltpu.make_async_copy(k.ACC.at[it, s], gr_o.at[it], k.OS.at[lax.rem(order(v, c, n), d.NSX)])
+
+    def begin(i, v, c, n):
         if i == last:
-            out_copy(c).start()
+            out_copy(v, c, n).start()
             return
-        src, dst, (ss, rs), peer, _ = stage(i, c)
-        if i >= d.first_ag:
-            pl.semaphore_wait(k.CR.at[i - d.first_ag], 1)
-        remote(src, dst, ss, rs, peer).start()
-
-    def finish(i, c):
+        copies, _, _ = stage(i, v, c, n)
+        slot = lax.rem(order(v, c, n), d.NS[i])
+        for at, (src, dst, peer, credit) in enumerate(copies):
+            if i >= d.first_ag:
+                pl.semaphore_wait(k.CR.at[credit], 1)
+            remote(src, dst, k.SS.at[i, slot, at], k.SR.at[i, slot, at], peer).start()
+
+    def finish(i, v, c, n):
         if i == last:
-            out_copy(c).wait()
+            out_copy(v, c, n).wait()
             return
-        src, dst, (ss, rs), peer, add = stage(i, c)
-        remote(src, dst, ss, rs, peer).wait()
-        if add is not None:
-            add[0][...] = add[0][...] + add[1][...]
-        if i in credit_of:
-            pl.semaphore_signal(k.CR.at[credit_of[i]], inc=1, device_id=peer, device_id_type=MESH)
-
-    credit_of = {4: 0, 3: 1, 2: 2, 0: 3}
-
-    def tick(t):
-        for i in range(last, -1, -1):
-            c, ok = chunk_of(t - d.E[i])
-            guarded(ok, functools.partial(finish, i, c))
-        for i in range(last, -1, -1):
-            c, ok = chunk_of(t - d.B[i])
-            guarded(ok, functools.partial(begin, i, c))
+        copies, target, terms = stage(i, v, c, n)
+        slot = lax.rem(order(v, c, n), d.NS[i])
+        for at, (src, dst, peer, credit) in enumerate(copies):
+            remote(src, dst, k.SS.at[i, slot, at], k.SR.at[i, slot, at], peer).wait()
+        if terms is not None:
+            total = target[...].astype(F32) + terms[0][...].astype(F32)
+            for term in terms[1:]:
+                total = total + term[...].astype(F32)
+            target[...] = total.astype(BF16)
+            for _, _, peer, credit in copies:
+                if credit is not None:
+                    pl.semaphore_signal(k.CR.at[credit], inc=1, device_id=peer, device_id_type=MESH)
+
+    def tick(t, kinds=(2, 1)):
+        for what, ticks in ((finish, d.E), (begin, d.B)):
+            for i in range(last, -1, -1):
+                v = t - ticks[i]
+                for cond, c, n in chunks_of(v, kinds):
+                    guarded(cond, functools.partial(what, i, v, c, n))
 
     def put_cols(c, sh, value):
         value = value.astype(BF16)
@@ -546,10 +567,10 @@
         k.VG[1, :, at] = total[:, LANES:]
         for n in range(d.NP):
             put_out(2 * j, n, nn(k.ACTT[...], k.COT[:, n * BLK:(n + 1) * BLK]))
-        tick(2 * j)
         for sh in range(2):
-            put_cols(2 * j + 1, sh, nn(k.N2T[sh * d.DH:(sh + 1) * d.DH, :], k.DPRE[...]))
-        tick(2 * j + 1)
+            row = pl.ds(sh * d.DH, d.DH)
+            put_cols(2 * j + 1, sh, nn(k.N2T[row, :], k.DPRE[...]))
+        tick(j, (2,))
         return 0
 
     lax.fori_loop(0, d.NJ, mlp, 0)
@@ -587,7 +608,7 @@
         cols = pl.ds(pl.multiple_of(n * BLK, BLK), BLK)
         for sh in range(2):
             put_cols(c, sh, nn(k.N2T[sh * d.DH:(sh + 1) * d.DH, :], k.N2[:, cols]))
-        tick(c)
+        tick(d.NJ + n)
         return 0
 
     lax.fori_loop(0, d.NP, proj_cols, 0)
@@ -659,7 +680,7 @@
         k.VG[half, :, at:at + n] = jnp.zeros((1, n), F32)
 
     def group(grp, _):
-        v0 = d.V0 + grp * d.GV
+        v0 = d.V0 + grp * d.GU
 
         def unit(u, _):
             attend_back(lax.div(u, 2), 2 * grp + lax.rem(u, 2))
@@ -669,12 +690,11 @@
         lax.fori_loop(0, d.GU, unit, 0)
 
         def part_step(part, _):
-            c = d.V0 + 3 * grp + part
+            c = 2 * d.NJ + d.NP + 3 * grp + part
             cols = pl.ds(pl.multiple_of(part * d.D + grp * BLK, BLK), BLK)
             for sh in range(2):
                 put_cols(c, sh, nn(k.N2T[sh * d.DH:(sh + 1) * d.DH, :], k.QKV[:, cols]))
 
-            tick(v0 + d.GU + part)
             return 0
 
         lax.fori_loop(0, 3, part_step, 0)
@@ -682,11 +702,11 @@
 
     lax.fori_loop(0, d.NP, group, 0)
 
-    HB, TB = 256, 2
+    HB = 256
     NB = d.M // HB
 
-    def norm1_back(i, sums):
-        rows = pl.ds(pl.multiple_of(i * HB, HB), HB)
+    def norm1_back(i):
+        rows = pl.ds(i * HB, HB)
         dn = nt(k.QKV[rows, :], k.WQ[...])
         xhat, r = norm_rows(k.T[rows, :].astype(F32))
         gg = dn * g1
@@ -694,16 +714,13 @@
             gg - jnp.mean(gg, axis=-1, keepdims=True) - xhat * jnp.mean(gg * xhat, axis=-1, keepdims=True)
         )
         k.COT[rows, :] = dx.astype(BF16)
-        add = lambda v: jnp.sum(v, axis=0, keepdims=True)
-        for u in range(TB):
-            tick(d.NVS + TB * i + u)
-        return sums[0] + add(dn * xhat), sums[1] + add(dn)
-
-    sums = lax.fori_loop(0, NB, norm1_back, (zrow, zrow))
-    put_vec("ln1g", sums[0])
-    put_vec("ln1b", sums[1])
-    xcopy = pltpu.make_async_copy(k.COT, dx_o, k.LS.at[0])
-    xcopy.start()
+        return jnp.sum(dn * xhat, axis=0, keepdims=True), jnp.sum(dn, axis=0, keepdims=True)
+
+    bout = full("outb")
+
+    def out_rows(i):
+        rows = pl.ds(i * HB, HB)
+        k.N2[rows, :] = (k.HRES[rows, :] + nn(k.ACT[rows, :], k.WO[...]) + bout).astype(BF16)
 
     def vec_copy(i):
         src = k.VG.at[o] if i == 0 else k.VG.at[s]
@@ -711,39 +728,32 @@
         return remote(src, k.VR.at[i], k.VS.at[i], k.VQ.at[i], peer)
 
     n_v = d.nb + 1
-
-    def vec_step(i):
-        vec_copy(i).wait()
-        k.VG[s] = k.VG[s] + k.VR[i]
-        if i + 1 < n_v:
-            vec_copy(i + 1).start()
-
-    vec_copy(0).start()
-    bout = full("outb")
-
-    def out_step(i, _):
-        @pl.when(i < NB)
-        def _():
-            rows = pl.ds(pl.multiple_of(i * HB, HB), HB)
-            y = k.HRES[rows, :] + nn(k.ACT[rows, :], k.WO[...]) + bout
-            k.N2[rows, :] = y.astype(BF16)
-
-        for u in range(TB):
-            tick(d.NVS + TB * (NB + i) + u)
-        for v in range(n_v):
-            pl.when(i == v)(functools.partial(vec_step, v))
-        return 0
-
-    n_out = max(NB, n_v)
-    lax.fori_loop(0, n_out, out_step, 0)
+    xcopy = pltpu.make_async_copy(k.COT, dx_o, k.LS.at[0])
     bcopy = pltpu.make_async_copy(k.N2, out_o, k.LS.at[1])
-    bcopy.start()
-
-    def rest(t, _):
+    at_block, at_vec, sums = 0, 0, (zrow, zrow)
+    for t in range(d.VD, d.NVS + d.E[-1]):
         tick(t)
-        return 0
-
-    lax.fori_loop(d.NVS + TB * (NB + n_out), d.NVS + d.E[-1], rest, 0)
+        if at_block > NB and at_vec < n_v:
+            vec_copy(at_vec).wait()
+            k.VG[s] = k.VG[s] + k.VR[at_vec]
+            at_vec += 1
+            if at_vec < n_v:
+                vec_copy(at_vec).start()
+        for _ in range(DRAIN[t - d.VD] if t - d.VD < len(DRAIN) else 2 * NB):
+            if at_block < NB:
+                a, b = norm1_back(at_block)
+                sums = sums[0] + a, sums[1] + b
+                if at_block == NB - 1:
+                    put_vec("ln1g", sums[0])
+                    put_vec("ln1b", sums[1])
+                    xcopy.start()
+                    vec_copy(0).start()
+            elif at_block < 2 * NB:
+                out_rows(at_block - NB)
+                if at_block == 2 * NB - 1:
+                    bcopy.start()
+            at_block += 1
+    assert at_block >= 2 * NB and at_vec == n_v
     vo_o[...] = k.VG[s]
     xcopy.wait()
     bcopy.wait()

time: 207 us -> 199 us (0.961)
  Pallas kernels: 201 us -> 193 us
    pallas_call x1, Pallas kernels: 192 us -> 184 us  [per_device(): pl.pallas_call(functools.partial(block_kernel, d, names), out_shape=(jax....]
where the time goes in v4:
time: 199 us
  Pallas kernels  193 us (97%)
  local copies, waits for them, and re-layouts  4.54 us (2%)
    pallas_call x1, Pallas kernels, per_device(): pl.pallas_call(functools.partial(block_kernel, d, names), out_shape=(jax....  184 us
    pallas_call x1, Pallas kernels, per_device(): pl.pallas_call(functools.partial(finish_kernel, d), out_shape=tuple((jax....  8.85 us

profile of v4, /device:TPU:0, one launch (start us, length us, event | category | flops | bytes accessed | tf_op | source)
XLA Modules:
  0.0 198.8 jit_solution(5536486435609964907)
XLA Ops:
  0.6 0.8 convert_add_fusion
  1.5 0.6 reshape.31.vec
  2.1 183.9 %block.1 = (bf16[1024,768]{1,0:T(8,128)(2,1)}, bf16[1024,768]{1,0:T(8,128)(2,1)}, bf16[36,8,2,48,128]{4,3,2,1,0:T(8,128)(2,1)}, f32[1,4608]{1,0:T(1,128)}) custom-call(bf16[1024,768]{1,0:T(8,128)(2,1)} %tok.1, bf16[1024,768]{1,0:T(8,128)(2,1)} %cot.1, bf16[384,2304]{1,0:T(8,128)(2,1)} %wq.1, bf16[384,768]{1,0:T(8,128)(2,1)} %wp.1, bf16[384,3072]{1,0:T(8,128)(2,1)} %wf.1, ...), custom_call_target="tpu_custom_call" | custom-call | tf_op jit(solution)/shard_map/block/pallas_call | solution.py:770
  186.0 8.9 %finish.1 = (f32[384,2304]{1,0:T(8,128)}, f32[384,768]{1,0:T(8,128)}, f32[384,3072]{1,0:T(8,128)}, f32[1536,768]{1,0:T(8,128)}, f32[384]{0:T(512)}, /*index=5*/f...) custom-call(bf16[36,8,2,48,128]{4,3,2,1,0:T(8,128)(2,1)} %get-tuple-, ...), custom_call_target="tpu_custom_call" | custom-call | tf_op jit(solution)/shard_map/finish/pallas_call | solution.py:787
  194.9 0.0 copy-start
  194.9 2.8 %copy.30 = bf16[1024,768]{1,0:T(8,128)(2,1)} copy(bf16[1024,768]{1,0:T(8,128)(2,1)} %get-tuple-element.60) | data formatting | bytes 3145728
  197.7 0.0 copy-done
  197.7 1.1 copy.31
Async XLA Ops:
  194.9 2.8 %copy-start = (bf16[1024,768]{1,0:T(8,128)(2,1)S(1)}, bf16[1024,768]{1,0:T(8,128)(2,1)}, u32[]{:S(2)}) copy-start(bf16[1024,768]{1,0:T(8,128)(2,1)} %get-tuple-element.61) | copy-start | bytes 4718596

commit v5 on v4

--- a/solution.py
+++ b/solution.py
@@ -17,7 +17,7 @@
 LANES = 128
 BLK = 256
 NEG = -1e30
-DRAIN = (0, 0, 2, 1, 1, 1, 1, 1, 1)
+DRAIN = (0, 0, 1, 1, 1, 1, 1, 1, 1, 1)
 VECS = ("ln1g", "ln1b", "qvb", "projb", "ln2g", "ln2b", "outb", "fcb")
 
 
@@ -603,22 +603,16 @@
 
     lax.fori_loop(0, d.M // HA, transpose_att, 0)
 
-    def proj_cols(n, _):
+    def proj_cols(n):
         c = 2 * d.NJ + n
-        cols = pl.ds(pl.multiple_of(n * BLK, BLK), BLK)
+        cols = pl.ds(n * BLK, BLK)
         for sh in range(2):
             put_cols(c, sh, nn(k.N2T[sh * d.DH:(sh + 1) * d.DH, :], k.N2[:, cols]))
-        tick(d.NJ + n)
-        return 0
-
-    lax.fori_loop(0, d.NP, proj_cols, 0)
 
     def att_rows(i, _):
         rows = pl.ds(pl.multiple_of(i * RB, RB), RB)
         k.N1[rows, :] = nt(k.N2[rows, :], k.WP[...]).astype(BF16)
         return 0
-
-    lax.fori_loop(0, d.M // RB, att_rows, 0)
 
     g1, be1 = full("ln1g"), full("ln1b")
 
@@ -628,7 +622,13 @@
         k.N2T[:, rows] = (xhat * g1 + be1).astype(BF16).T
         return 0
 
-    lax.fori_loop(0, d.M // HA, transpose_n1, 0)
+    parts = [-(-n * (d.M // RB) // d.NP) for n in range(d.NP + 1)]
+    for n in range(d.NP):
+        proj_cols(n)
+        if n == d.NP - 1:
+            lax.fori_loop(0, d.M // HA, transpose_n1, 0)
+        tick(d.NJ + n)
+        lax.fori_loop(parts[n], parts[n + 1], att_rows, 0)
 
     def attend_back(seq, hp):
         rows, cols = unit_refs(seq, hp)
@@ -784,24 +784,26 @@
         name="block",
     )(tok, cot, wq, wp, wf, wo, vec)
     vecs_out = tuple(jax.ShapeDtypeStruct((n,), F32) for _, n in d.off.values())
-    g_q, g_p, g_fc, g_out, *v = pl.pallas_call(
+    out, dx, g_q, g_p, g_fc, g_out, *v = pl.pallas_call(
         functools.partial(finish_kernel, d),
-        out_shape=tuple(
+        out_shape=(jax.ShapeDtypeStruct((d.M, d.D), BF16),) * 2 + tuple(
             jax.ShapeDtypeStruct(shape, F32)
             for shape in ((d.DH, 3 * d.D), (d.DH, d.D), (d.DH, d.FF), (d.FH, d.D))
         ) + vecs_out,
-        in_specs=[hbm, vmem],
-        out_specs=(hbm,) * 4 + (vmem,) * len(vecs_out),
+        in_specs=[hbm] * 3 + [vmem],
+        out_specs=(hbm,) * 6 + (vmem,) * len(vecs_out),
         scratch_shapes=[
             pltpu.VMEM((d.NCH, 8, 2, d.PR, LANES), BF16),
             pltpu.VMEM((2 * d.NJ + 8 * d.NP, d.DH, LANES), F32),
             pltpu.VMEM((d.NJ, LANES, d.D), F32),
+            pltpu.VMEM((2, d.M, d.D), BF16),
             pltpu.SemaphoreType.DMA((d.NCH,)),
             pltpu.SemaphoreType.DMA((d.NCH,)),
+            pltpu.SemaphoreType.DMA((4,)),
         ],
         compiler_params=pltpu.CompilerParams(vmem_limit_bytes=67_043_328),
         name="finish",
-    )(gr, vo)
+    )(out, dx, gr, vo)
     v = dict(zip(d.off, v))
     return (
         out, dx, v["ln1g"], v["ln1b"], g_q, v["qvb"], g_p, v["projb"],
@@ -809,8 +811,8 @@
     )
 
 
-def finish_kernel(d, gr, vo, g_q, g_p, g_fc, g_out, *refs):
-    outs, (G, C, O, si, so) = refs[:len(d.off)], refs[len(d.off):]
+def finish_kernel(d, out_i, dx_i, gr, vo, out_o, dx_o, g_q, g_p, g_fc, g_out, *refs):
+    outs, (G, C, O, X, si, so, sx) = refs[:len(d.off)], refs[len(d.off):]
     for ref, (at, n) in zip(outs, d.off.values()):
         ref[...] = vo[0, at:at + n]
 
@@ -819,6 +821,10 @@
         return 0
 
     lax.fori_loop(0, d.NCH, load, 0)
+    rows_in = [pltpu.make_async_copy(r, X.at[i], sx.at[i]) for i, r in enumerate((out_i, dx_i))]
+    rows_out = [pltpu.make_async_copy(X.at[i], r, sx.at[2 + i]) for i, r in enumerate((out_o, dx_o))]
+    for copy in rows_in:
+        copy.start()
 
     def arrived(c):
         pltpu.make_async_copy(gr.at[c], G.at[c], si.at[c]).wait()
@@ -866,6 +872,9 @@
         return 0
 
     lax.fori_loop(0, d.NJ, mlp, 0)
+    for a, b in zip(rows_in, rows_out):
+        a.wait()
+        b.start()
     for i in range(4 * d.NP):
         cols_of(2 * d.NJ + i, 2 * (d.NJ + i))
         for copy in wide_copies(i):
@@ -878,6 +887,8 @@
         return 0
 
     lax.fori_loop(0, d.NJ, drain, 0)
+    for copy in rows_out:
+        copy.wait()
     for i in range(4 * d.NP):
         pair = C.at[pl.ds(0, 2)]
         pltpu.make_async_copy(pair, pair, so.at[2 * d.NJ + i]).wait()

time: 199 us -> 199 us (level)
  local copies, waits for them, and re-layouts: 4.54 us -> 0.62 us
  Pallas kernels: 193 us -> 196 us
    unnamed x4 -> x0, local copies, waits for them, and re-layouts: 3.92 us -> none
    pallas_call x1, Pallas kernels: 8.85 us -> 12.1 us  [per_device(): pl.pallas_call(functools.partial(finish_kernel, d), out_shape=(jax.ShapeD...]
where the time goes in v5:
time: 199 us; the launch traced here: 198 us
  Pallas kernels  196 us (98%)
    pallas_call x1, Pallas kernels, per_device(): pl.pallas_call(functools.partial(block_kernel, d, names), out_shape=(jax....  184 us
    pallas_call x1, Pallas kernels, per_device(): pl.pallas_call(functools.partial(finish_kernel, d), out_shape=(jax.ShapeD...  12.1 us

profile of v5, /device:TPU:0, one launch (start us, length us, event | category | flops | bytes accessed | tf_op | source)
XLA Modules:
  0.0 198.3 jit_solution(394525761565732811)
XLA Ops:
  0.6 0.8 convert_add_fusion
  1.5 0.6 reshape.31.vec
  2.1 184.0 %block.1 = (bf16[1024,768]{1,0:T(8,128)(2,1)}, bf16[1024,768]{1,0:T(8,128)(2,1)}, bf16[36,8,2,48,128]{4,3,2,1,0:T(8,128)(2,1)}, f32[1,4608]{1,0:T(1,128)}) custom-call(bf16[1024,768]{1,0:T(8,128)(2,1)} %tok.1, bf16[1024,768]{1,0:T(8,128)(2,1)} %cot.1, bf16[384,2304]{1,0:T(8,128)(2,1)} %wq.1, bf16[384,768]{1,0:T(8,128)(2,1)} %wp.1, bf16[384,3072]{1,0:T(8,128)(2,1)} %wf.1, ...), custom_call_target="tpu_custom_call" | custom-call | tf_op jit(solution)/shard_map/block/pallas_call | solution.py:770
  186.0 12.1 %finish.1 = (bf16[1024,768]{1,0:T(8,128)(2,1)}, bf16[1024,768]{1,0:T(8,128)(2,1)}, f32[384,2304]{1,0:T(8,128)}, f32[384,768]{1,0:T(8,128)}, f32[384,3072]{1,0:T(...) custom-call(bf16[1024,768]{1,0:T(8,128)(2,1)} %get-tuple-element.32., ...), custom_call_target="tpu_custom_call" | custom-call | tf_op jit(solution)/shard_map/finish/pallas_call | solution.py:787
